TPU v7x, 128 devices: a whole 4x4x4 slice. The times are simulated.
128 devices in a mesh: cache: 16 (over x, z), expert: 8 (over y, core).
Axes of the slice: x: 4, y: 4, z: 4, core: 2. Of those that a mesh axis runs over, the one named last changes fastest.
Arguments:
- query: bfloat16 [1024, 4096], P('cache', 'expert'), may hold values from -8 to 8
- new_key: bfloat16 [1024, 1024], P('cache', 'expert'), may hold values from -8 to 8
- new_value: bfloat16 [1024, 1024], P('cache', 'expert'), may hold values from -6 to 6
- private_keys: bfloat16 [1024, 64, 1024], P('cache', None, 'expert'), may hold values from -8 to 8
- private_values: bfloat16 [1024, 64, 1024], P('cache', None, 'expert'), may hold values from -6 to 6
- private_lengths: int32 [1024], P('cache'), may hold values from 1 to 64
- prefix_keys: bfloat16 [32, 1024, 1024], P('cache', None, 'expert'), may hold values from -8 to 8
- prefix_values: bfloat16 [32, 1024, 1024], P('cache', None, 'expert'), may hold values from -6 to 6
- slot_group: int32 [32], replicated, may hold values from 0 to 31, each once
- group_ids: int32 [1024, 1], P('cache'), may hold values from 0 to 31; in each aligned block of 64 rows (0 to 63, 64 to 127, ...) at most 8 rows name the same one
- out_weight: bfloat16 [4096, 4096], P('expert', 'cache'), may hold values from -0.09375 to 0.09375
- hidden_in: bfloat16 [1024, 4096], P(('cache', 'expert')), may hold values from -6 to 6
- norm_gain: float32 [4096], replicated, may hold values from 0.1 to 1.9
- expert_ids: int32 [1024, 2], P(('cache', 'expert')), may hold values from 0 to 7, all different within a row; in each aligned block of 8 rows (0 to 7, 8 to 15, ...) at most 4 rows name the same one
- gate_weights: float32 [1024, 2], P(('cache', 'expert')), may hold values from 0.1 to 0.9
- w_gate: bfloat16 [8, 4096, 14336], P('expert', None, 'cache'), may hold values from -0.09375 to 0.09375
- w_up: bfloat16 [8, 4096, 14336], P('expert', None, 'cache'), may hold values from -0.09375 to 0.09375
- w_down: bfloat16 [8, 14336, 4096], P('expert', 'cache'), may hold values from -0.046875 to 0.046875
Outputs:
- attention: bfloat16 [1024, 4096], P('cache', 'expert')
- layer_out: bfloat16 [1024, 4096], P(('cache', 'expert'))
Inputs may be any that keep to these rules, and one draw needn't show every extreme that they name: `group_ids`: within each aligned block of 64 requests at most 8 name one group. `slot_group`: each group is held by exactly one slot. `private_lengths`: positions 0 to length - 1 of a request's private cache are live. `expert_ids`: each token names two different experts; among the 8 tokens of one device at most 4 name one expert.
All inputs are finite; a program needn't handle non-finite values.
Results may differ from a plain program's by a relative error of at most 0.0095.
Values may be sent and summed in bfloat16 or wider, within the bound.
No kernel may reach another device: no remote copies, remote signals or barrier semaphores. Data moves between devices by JAX's collectives and lax.ppermute only.
A program may use at most 128 MiB of HBM per device.

v0:
```python
import math

import jax
import jax.numpy as jnp
from jax import lax
from jax.experimental import pallas as pl
from jax.experimental.pallas import tpu as pltpu
from jax.sharding import Mesh
from jax.sharding import PartitionSpec as P

MOSTG = 8
CACHE = ("x", "z")
CACHE_EXPERT = ("x", "z", "y", "k")
RING = 4
VLIM = 16
N_BLOCK = 1024

NEG = -1e30
EPSILON = 1e-05
F32 = jnp.float32
BF16 = jnp.bfloat16


def push(block, axis, distance):
    if distance == 0:
        return block
    return lax.ppermute(block, axis, [(i, (i + distance) % RING) for i in range(RING)])


def turn(block, stage, distance):
    if distance == 0:
        return block
    pairs = []
    for x in range(RING):
        for z in range(RING):
            for k in range(2):
                along_x = (k + stage) % 2 == 0
                to_x = (x + distance) % RING if along_x else x
                to_z = z if along_x else (z + distance) % RING
                pairs.append(((x * RING + z) * 2 + k, (to_x * RING + to_z) * 2 + k))
    return lax.ppermute(block, ("x", "z", "k"), pairs)


def swap(block):
    return lax.ppermute(block, "k", [(0, 1), (1, 0)])


def private_partial(queries, keys, values, lengths, new_key, new_value, scale):
    scores = jnp.einsum("rhd,rpd->rhp", queries, keys, preferred_element_type=F32) * scale
    live = jnp.arange(keys.shape[1], dtype=jnp.int32)[None, :] < lengths[:, None]
    scores = jnp.where(live[:, None, :], scores, NEG)
    fresh = jnp.einsum("rhd,rd->rh", queries, new_key, preferred_element_type=F32) * scale
    top = jnp.maximum(jnp.max(scores, axis=-1), fresh)
    expo = jnp.where(live[:, None, :], jnp.exp(scores - top[..., None]), 0.0)
    fresh_expo = jnp.exp(fresh - top)
    total = jnp.sum(expo, axis=-1) + fresh_expo
    summed = jnp.einsum("rhp,rpd->rhd", expo.astype(BF16), values, preferred_element_type=F32)
    summed = summed + fresh_expo[..., None] * new_value.astype(F32)[:, None, :]
    return (summed / total[..., None], top + jnp.log(total))


def in_pieces(value):
    first = lax.reduce_precision(value, 8, 7)
    rest = value - first
    second = lax.reduce_precision(rest, 8, 7)
    return (first, second, rest - second)


def prefix_kernel(heads, width, scale, received, keys, values, out):
    rows = received[...].astype(F32).reshape(-1, heads * width).astype(BF16)
    count = rows.shape[0]
    queries = jnp.concatenate([rows[:, h * width : (h + 1) * width] for h in range(heads)], axis=0)
    scores = lax.dot_general(
        queries, keys[0], (((1,), (1,)), ((), ())), preferred_element_type=F32
    )
    scores = scores * scale
    top = jnp.max(scores, axis=-1, keepdims=True)
    expo = jnp.exp(scores - top)
    total = jnp.sum(expo, axis=-1, keepdims=True)
    summed = jnp.dot(expo.astype(BF16), values[0], preferred_element_type=F32)
    outputs = summed / total
    parts = in_pieces(top + jnp.log(total))
    lane = lax.broadcasted_iota(jnp.int32, (count, width), 1)
    packed = jnp.zeros((count, width), F32)
    for p, part in enumerate(parts):
        for h in range(heads):
            packed = jnp.where(lane == p * heads + h, part[h * count : (h + 1) * count], packed)
    for h in range(heads):
        block = outputs[h * count : (h + 1) * count].reshape(-1, 1, MOSTG, width)
        out[:, :, :, h * width : (h + 1) * width] = block.astype(BF16)
    out[:, :, :, heads * width :] = packed.reshape(-1, 1, MOSTG, width).astype(BF16)


def prefix_partial(received, keys, values, heads, scale):
    slots, length, width = keys.shape
    homes = received.shape[0] // (slots * MOSTG)
    return pl.pallas_call(
        lambda *refs: prefix_kernel(heads, width, scale, *refs),
        grid=(slots,),
        in_specs=[
            pl.BlockSpec((homes, 1, MOSTG, heads * width), lambda g: (0, g, 0, 0)),
            pl.BlockSpec((1, length, width), lambda g: (g, 0, 0)),
            pl.BlockSpec((1, length, width), lambda g: (g, 0, 0)),
        ],
        out_specs=pl.BlockSpec((homes, 1, MOSTG, (heads + 1) * width), lambda g: (0, g, 0, 0)),
        out_shape=jax.ShapeDtypeStruct((homes, slots, MOSTG, (heads + 1) * width), BF16),
        compiler_params=pltpu.CompilerParams(vmem_limit_bytes=24 * 1024 * 1024),
        name="prefix_attention",
    )(
        received.reshape(homes, slots, MOSTG, heads * width),
        pltpu.with_memory_space_constraint(keys, pltpu.HBM),
        pltpu.with_memory_space_constraint(values, pltpu.HBM),
    ).reshape(
        homes * slots * MOSTG, (heads + 1) * width
    )


def expert_kernel(count, *refs):
    pieces = refs[:count]
    w_gate, w_up, w_down = refs[count : count + 3]
    outs = refs[count + 4 :]
    rows = jnp.concatenate([piece[...] for piece in pieces], axis=0)
    gate = jnp.dot(rows, w_gate[...], preferred_element_type=F32)
    up = jnp.dot(rows, w_up[...], preferred_element_type=F32)
    act = (gate / (1.0 + jnp.exp(-gate)) * up).astype(BF16)
    size = rows.shape[0] // count
    for n in range(0, w_down.shape[1], N_BLOCK):
        out = jnp.dot(act, w_down[:, n : n + N_BLOCK], preferred_element_type=F32).astype(BF16)
        for i in range(count):
            outs[i][:, n : n + N_BLOCK] = out[i * size : (i + 1) * size]


def apply_expert(pieces, weights, token):
    count = len(pieces)
    local = pl.BlockSpec(memory_space=pltpu.VMEM)
    return pl.pallas_call(
        lambda *refs: expert_kernel(count, *refs),
        in_specs=[local] * (count + 3) + [pl.BlockSpec(memory_space=pl.ANY)],
        out_specs=[local] * count,
        out_shape=[jax.ShapeDtypeStruct(pieces[0].shape, BF16)] * count,
        compiler_params=pltpu.CompilerParams(vmem_limit_bytes=VLIM * 1024 * 1024),
        name="expert_rows",
    )(*pieces, *weights, token)


def project_kernel(count, other, *refs):
    pieces = refs[:count]
    weights = refs[count : 2 * count]
    sent = refs[2 * count]
    kept = refs[2 * count + 1 :]
    for side in range(2):
        rows = jnp.concatenate([piece[side] for piece in pieces], axis=0)
        for j in range(count):
            wide = weights[j].shape[1]
            terms = jnp.dot(rows, weights[j][...], preferred_element_type=F32)
            terms = terms.reshape(count, count, -1, wide)
            for y in range(count):
                if side == other:
                    sent[y, :, :, j * wide : (j + 1) * wide] = terms[:, y].astype(BF16)
                else:
                    kept[y][:, :, j * wide : (j + 1) * wide] = terms[:, y]


def project(pieces, weights):
    count = len(pieces)
    tokens = pieces[0].shape[1] // count
    wide = sum(w.shape[1] for w in weights)
    local = pl.BlockSpec(memory_space=pltpu.VMEM)
    return pl.pallas_call(
        lambda *refs: project_kernel(count, 1, *refs),
        in_specs=[local] * (2 * count),
        out_specs=[local] * (count + 1),
        out_shape=[jax.ShapeDtypeStruct((count, count, tokens, wide), BF16)]
        + [jax.ShapeDtypeStruct((count, tokens, wide), F32)] * count,
        compiler_params=pltpu.CompilerParams(vmem_limit_bytes=16 * 1024 * 1024),
        name="project_rows",
    )(*pieces, *weights)


def load_kernel(count, *refs):
    sources, outs, sems = refs[:count], refs[count + 1 : 2 * count + 1], refs[2 * count + 1]
    copies = [
        pltpu.make_async_copy(sources[i], outs[i], sems.at[i]) for i in range(count)
    ]
    for copy in copies:
        copy.start()
    for copy in copies:
        copy.wait()


def loaded(weights, token):
    count = len(weights)
    far = pl.BlockSpec(memory_space=pl.ANY)
    outs = pl.pallas_call(
        lambda *refs: load_kernel(count, *refs),
        in_specs=[far] * (count + 1),
        out_specs=[pl.BlockSpec(memory_space=pltpu.VMEM)] * count,
        out_shape=[jax.ShapeDtypeStruct(w.shape, w.dtype) for w in weights],
        scratch_shapes=[pltpu.SemaphoreType.DMA((count,))],
        compiler_params=pltpu.CompilerParams(vmem_limit_bytes=4 * 1024 * 1024),
        name="load_weights",
    )(*[pltpu.with_memory_space_constraint(w, pltpu.HBM) for w in weights], token)
    return [pltpu.with_memory_space_constraint(w, pltpu.VMEM) for w in outs]


def on_device(
    query,
    new_key,
    new_value,
    private_keys,
    private_values,
    private_lengths,
    prefix_keys,
    prefix_values,
    slot_group,
    group_ids,
    out_weight,
    hidden_in,
    norm_gain,
    expert_ids,
    gate_weights,
    w_gate,
    w_up,
    w_down,
):
    at_x, at_z, at_y, at_k = (lax.axis_index(name) for name in CACHE_EXPERT)
    head_dim = new_key.shape[1]
    requests = query.shape[0]
    heads = query.shape[1] // head_dim
    width = heads * head_dim
    scale = 1.0 / math.sqrt(head_dim)
    experts = 2 * RING
    tokens = hidden_in.shape[0]

    slot_count = slot_group.shape[0]
    matches = group_ids[:, 0][:, None] == slot_group[None, :]
    slot = jnp.sum(jnp.where(matches, jnp.arange(slot_count, dtype=jnp.int32)[None, :], 0), axis=1)
    order = jnp.arange(requests, dtype=jnp.int32)
    earlier = order[None, :] < order[:, None]
    rank = jnp.sum((slot[:, None] == slot[None, :]) & earlier, axis=1)
    position = slot * MOSTG + rank
    places = jnp.arange(slot_count * MOSTG, dtype=jnp.int32)
    placing = (places[:, None] == position[None, :]).astype(BF16)
    sent = jnp.dot(placing, query, preferred_element_type=F32).astype(BF16)
    received = lax.all_to_all(sent, CACHE, split_axis=0, concat_axis=0, tiled=True)

    queries = query.reshape(requests, heads, head_dim)
    near_out, near_lse = private_partial(
        queries, private_keys, private_values, private_lengths, new_key, new_value, scale
    )

    partial = prefix_partial(received, prefix_keys, prefix_values, heads, scale)
    late_weight, partial = lax.optimization_barrier((out_weight, partial))
    back = lax.all_to_all(partial, CACHE, split_axis=0, concat_axis=0, tiled=True)

    weights = [push(late_weight, "x", -j) for j in range(RING)]

    taken = lax.dot_general(placing, back, (((0,), (0,)), ((), ())), preferred_element_type=F32)
    far_out = taken[:, :width].reshape(requests, heads, head_dim)
    far_lse = taken[:, width : width + 3 * heads].reshape(requests, 3, heads).sum(axis=1)
    both = jnp.logaddexp(near_lse, far_lse)
    merged = (
        near_out * jnp.exp(near_lse - both)[..., None]
        + far_out * jnp.exp(far_lse - both)[..., None]
    )
    attention = merged.astype(BF16).reshape(requests, width)

    rows = attention.reshape(RING, 2, tokens, width).transpose(1, 0, 2, 3)
    rows = jnp.where(at_k == 0, rows, rows[::-1])
    rows = lax.dynamic_slice_in_dim(jnp.concatenate([rows, rows], axis=1), at_y, RING, 1)
    rows = rows.reshape(2, RING * tokens, width)
    sent, *kept = project([push(rows, "z", i) for i in range(RING)], weights)
    sent = swap(sent)
    halved = [(kept[j] + sent[j].astype(F32)).astype(BF16) for j in range(RING)]
    reduced = sum(push(halved[j], "y", j).astype(F32) for j in range(RING)).astype(BF16)
    spread = jnp.stack([push(reduced[i], "z", -i) for i in range(RING)])
    spread = spread.reshape(RING, tokens, RING, -1)
    spread = lax.dynamic_slice_in_dim(
        jnp.concatenate([spread, spread]), (RING - at_z) % RING, RING, 0
    )
    spread = lax.dynamic_slice_in_dim(
        jnp.concatenate([spread, spread], axis=2), (RING - at_x) % RING, RING, 2
    )
    proj = spread.transpose(1, 2, 0, 3).reshape(tokens, -1).astype(F32)
    resid = hidden_in.astype(F32) + proj
    normed = (
        resid * lax.rsqrt(jnp.mean(resid * resid, axis=-1, keepdims=True) + EPSILON) * norm_gain
    ).astype(BF16)

    capacity = max(2, 4 * tokens // experts)
    flat_ids = expert_ids.reshape(-1)
    order_ids = jnp.arange(flat_ids.shape[0], dtype=jnp.int32)
    before = order_ids[None, :] < order_ids[:, None]
    slot_rank = jnp.sum((flat_ids[:, None] == flat_ids[None, :]) & before, axis=1)
    away = (flat_ids // 2 - at_y) % RING
    other = (flat_ids % 2 + at_k) % 2
    destination = (away * 2 + other) * capacity + slot_rank
    expert_slots = jnp.arange(experts * capacity, dtype=jnp.int32)
    chosen = (destination[None, :] == expert_slots[:, None]).reshape(experts * capacity, tokens, 2)
    picking = jnp.sum(chosen.astype(BF16), axis=2)
    outgoing = jnp.dot(picking, normed, preferred_element_type=F32).astype(BF16)
    outgoing = outgoing.reshape(RING, 2, capacity, -1)
    own = jnp.stack([outgoing[:, 0], swap(outgoing[:, 1])], axis=1)
    arrived = jnp.stack([push(own[j], "y", j) for j in range(RING)])
    arrived = arrived.reshape(experts * capacity, -1)

    stacked = jnp.stack([turn(arrived, 0, j) for j in range(RING)])
    near = loaded([w_gate[0], w_up[0], w_down[0]], stacked)
    rows = stacked.reshape(-1, stacked.shape[-1])
    half = rows.shape[0] // 2
    low = turn(rows, 1, 1)
    high = turn(rows, 1, -1)
    (here_out,) = apply_expert([rows], near, norm_gain)
    low, high, here_out = lax.optimization_barrier((low, high, here_out))
    across = [turn(low[:half], 1, 1), turn(high[half:], 1, -1)]
    (low_out,) = apply_expert([low], near, here_out)
    (high_out,) = apply_expert([high], near, low_out)
    across_out = apply_expert(across, near, high_out)
    from_high = turn(across_out[0], 1, -1)
    from_low = turn(across_out[1], 1, 1)
    low_out = jnp.concatenate([low_out[:half] + from_high, low_out[half:]])
    high_out = jnp.concatenate([high_out[:half], high_out[half:] + from_low])
    summed = (
        here_out.astype(F32)
        + turn(low_out, 1, -1).astype(F32)
        + turn(high_out, 1, 1).astype(F32)
    )
    summed = summed.astype(BF16).reshape(stacked.shape)
    summed = sum(turn(summed[j], 0, -j).astype(F32) for j in range(RING)).astype(BF16)
    summed = summed.reshape(RING, 2, capacity, -1)

    own = jnp.stack([push(summed[j], "y", -j) for j in range(RING)])
    returned = jnp.stack([own[:, 0], swap(own[:, 1])], axis=1).reshape(experts * capacity, -1)
    mixing = jnp.sum(jnp.where(chosen, gate_weights[None, :, :], 0.0), axis=2)
    moe = jnp.einsum("st,sd->td", mixing, returned.astype(F32), precision=lax.Precision.HIGHEST)
    layer_out = (resid + moe).astype(BF16)
    return (attention, layer_out)


def solution(mesh):
    split = Mesh(mesh.devices.reshape(RING, RING, RING, 2), CACHE_EXPERT)
    expert = ("y", "k")
    in_specs = (
        P(CACHE, expert),
        P(CACHE, expert),
        P(CACHE, expert),
        P(CACHE, None, expert),
        P(CACHE, None, expert),
        P(CACHE),
        P(CACHE, None, expert),
        P(CACHE, None, expert),
        P(),
        P(CACHE, None),
        P(expert, CACHE),
        P(CACHE_EXPERT, None),
        P(),
        P(CACHE_EXPERT, None),
        P(CACHE_EXPERT, None),
        P(expert, None, CACHE),
        P(expert, None, CACHE),
        P(expert, CACHE, None),
    )
    out_specs = (P(CACHE, expert), P(CACHE_EXPERT, None))
    return jax.shard_map(
        on_device, mesh=split, in_specs=in_specs, out_specs=out_specs, check_vma=False
    )
```

profile of v0, /device:TPU:1, one launch (start us, length us, event | category | flops | bytes accessed | tf_op | source)
XLA Modules:
  0.0 179.7 jit_solution(13397186707062412521)
XLA Ops:
  1.7 1.7 convolution_convert_fusion.1
  3.4 8.4 %all-to-all-start = ((bf16[16,16,512]{2,1,0:T(8,128)(2,1)}), bf16[16,16,512]{2,1,0:T(8,128)(2,1)S(1)}, u32[]{:S(2)}, u32[]{:S(2)}) async-start(bf16[16,16,512]{2,1,0:T(8,128)(2,1)} %bitcast.3), calls=%async_computation | async-start | bytes 524288 | tf_op jit(solution)/shard_map/all_to_all | solution.py:245
  15.2 2.0 %fusion.51 = (f32[64,4]{1,0:T(8,128)S(1)}, f32[64,4,64]{2,1,0:T(4,128)S(1)}) fusion(bf16[64,4,128]{2,1,0:T(4,128)(2,1)S(1)} %reshape.204, bf16[64,64,128]{2,1,0:T(8,128)(2,1)} %param.21, pred[64,64]{1,0:T(8,128)(4,1)S(1)} %iota_compare_fusion.4), kind=kOutput, calls=%fused_computation.138 | convolution fusion | flops 4243200 | bytes 1184768 | tf_op jit(solution)/shard_map/rhd,rpd->rhp/dot_general | solution.py:49
  17.3 2.0 %all-to-all-done = bf16[16,16,512]{2,1,0:T(8,128)(2,1)S(1)} async-done(((bf16[16,16,512]{2,1,0:T(8,128)(2,1)}), bf16[16,16,512]{2,1,0:T(8,128)(2,1)S(1)}, u32[]{:S(2)}, u32[]{:S(2)}) %all-to-all-start) | async-done | bytes 262176 | tf_op jit(solution)/shard_map/all_to_all | solution.py:245
  19.3 5.1 %prefix_attention.1 = bf16[16,2,8,640]{3,2,1,0:T(8,128)(2,1)} custom-call(bf16[16,2,8,512]{3,2,1,0:T(8,128)(2,1)S(1)} %bitcast.100, bf16[2,1024,128]{2,1,0:T(8,128)(2,1)} %refs_1_.1, bf16[2,1024,128]{2,1,0:T(8,128)(2,1)} %refs_2_.1), custom_call_target="tpu_custom_call" | custom-call | tf_op jit(solution)/shard_map/prefix_attention/pallas_call | solution.py:97
  24.4 4.6 %all-to-all-start.1 = ((bf16[16,16,640]{2,1,0:T(8,128)(2,1)}), bf16[16,16,640]{2,1,0:T(8,128)(2,1)S(1)}, u32[]{:S(2)}, u32[]{:S(2)}) async-start(bf16[16,16,640]{2,1,0:T(8,128)(2,1)} %bitcast.6), calls=%async_computation.1 | async-start | bytes 655360 | tf_op jit(solution)/shard_map/all_to_all | solution.py:254
  29.5 1.4 collective-permute-start.5
  30.9 2.4 %collective-permute-start.4 = (bf16[512,256]{1,0:T(8,128)(2,1)S(1)}, bf16[512,256]{1,0:T(8,128)(2,1)S(1)}, u32[]{:S(2)}, u32[]{:S(2)}) collective-permute-start(bf16[512,256]{1,0:T(8,128)(2,1)S(1)} %copy-done.2), channel_id=1, source_target_pairs={{0,64},{32,96},{64,0},{96,32},{1,65},{33,97},{65,1},{97,33},{2,66}... | collective-permute-start | bytes 786440 | tf_op jit(solution)/shard_map/ppermute | solution.py:27
  33.3 1.2 collective-permute-start.3
  34.5 2.3 %all-to-all-done.1 = bf16[16,16,640]{2,1,0:T(8,128)(2,1)S(1)} async-done(((bf16[16,16,640]{2,1,0:T(8,128)(2,1)}), bf16[16,16,640]{2,1,0:T(8,128)(2,1)S(1)}, u32[]{:S(2)}, u32[]{:S(2)}) %all-to-all-start.1) | async-done | bytes 327712 | tf_op jit(solution)/shard_map/all_to_all | solution.py:254
  39.1 1.2 collective-permute-start.1
  40.3 1.2 collective-permute-done.5.refs_7_
  41.4 1.2 collective-permute-start
  42.8 3.3 %collective-permute-done.4.refs_6_ = bf16[512,256]{1,0:T(8,128)(2,1)S(1)} collective-permute-done((bf16[512,256]{1,0:T(8,128)(2,1)S(1)}, bf16[512,256]{1,0:T(8,128)(2,1)S(1)}, u32[]{:S(2)}, u32[]{:S(2)}) %collective-permute-start.4) | collective-permute-done | bytes 262176 | tf_op jit(solution)/shard_map/ppermute | solution.py:27
  46.6 4.0 %collective-permute-start.6 = (bf16[4,4,8,1024]{3,2,1,0:T(8,128)(2,1)S(1)}, bf16[4,4,8,1024]{3,2,1,0:T(8,128)(2,1)S(1)}, u32[]{:S(2)}, u32[]{:S(2)}) collective-permute-start(bf16[4,4,8,1024]{3,2,1,0:T(8,128)(2,1)S(1)} %get-tuple-element.20), channel_id=1, source_target_pairs={{0,1},{1,0},{2,3},{3,2},{4,5},{5,4},{6,7},{7,6},{8,9},{9,8},{10,11... | collective-permute-start | bytes 786440 | tf_op jit(solution)/shard_map/ppermute | solution.py:45
  51.8 1.4 collective-permute-start.7
  53.2 1.5 collective-permute-start.9
  54.7 1.6 collective-permute-start.8
  56.3 3.0 %collective-permute-done.8 = bf16[4,8,1024]{2,1,0:T(8,128)(2,1)S(1)} collective-permute-done((bf16[4,8,1024]{2,1,0:T(8,128)(2,1)S(1)}, bf16[4,8,1024]{2,1,0:T(8,128)(2,1)S(1)}, u32[]{:S(2)}, u32[]{:S(2)}) %collective-permute-start.8) | collective-permute-done | bytes 65568 | tf_op jit(solution)/shard_map/ppermute | solution.py:27
  59.5 2.1 %collective-permute-start.11 = (bf16[8,1024]{1,0:T(8,128)(2,1)S(1)}, bf16[8,1024]{1,0:T(8,128)(2,1)S(1)}, u32[]{:S(2)}, u32[]{:S(2)}) collective-permute-start(bf16[8,1024]{1,0:T(8,128)(2,1)S(1)} %get-tuple-element.58), channel_id=1, source_target_pairs={{0,16},{8,24},{16,0},{24,8},{1,17},{9,25},{17,1},{25,9},{2,18},{10... | collective-permute-start | bytes 49160 | tf_op jit(solution)/shard_map/ppermute | solution.py:27
  61.6 1.2 collective-permute-start.10
  62.8 1.4 collective-permute-done.10
  65.0 3.7 %collective-permute-start.13 = (bf16[4,4,4096]{2,1,0:T(4,128)(2,1)S(1)}, bf16[4,4,4096]{2,1,0:T(4,128)(2,1)S(1)}, u32[]{:S(2)}, u32[]{:S(2)}) collective-permute-start(bf16[4,4,4096]{2,1,0:T(4,128)(2,1)S(1)} %get-tuple-element.53), channel_id=1, source_target_pairs={{0,1},{1,0},{2,3},{3,2},{4,5},{5,4},{6,7},{7,6},{8,9},{9,8},{10,11... | collective-permute-start | bytes 393224 | tf_op jit(solution)/shard_map/ppermute | solution.py:45
  70.1 2.6 %collective-permute-start.16 = (bf16[2,4,4096]{2,1,0:T(4,128)(2,1)S(1)}, bf16[2,4,4096]{2,1,0:T(4,128)(2,1)S(1)}, u32[]{:S(2)}, u32[]{:S(2)}) collective-permute-start(bf16[2,4,4096]{2,1,0:T(4,128)(2,1)S(1)} %get-tuple-element.50), channel_id=1, source_target_pairs={{0,6},{2,0},{4,2},{6,4},{1,7},{3,1},{5,3},{7,5},{8,14},{10,8},{12,... | collective-permute-start | bytes 196616 | tf_op jit(solution)/shard_map/ppermute | solution.py:27
  73.2 1.2 collective-permute-done.14
  74.3 3.0 %collective-permute-done.15 = bf16[2,4,4096]{2,1,0:T(4,128)(2,1)S(1)} collective-permute-done((bf16[2,4,4096]{2,1,0:T(4,128)(2,1)S(1)}, bf16[2,4,4096]{2,1,0:T(4,128)(2,1)S(1)}, u32[]{:S(2)}, u32[]{:S(2)}) %collective-permute-start.15) | collective-permute-done | bytes 65568 | tf_op jit(solution)/shard_map/ppermute | solution.py:27
  77.6 2.5 %collective-permute-start.19 = (bf16[32,4096]{1,0:T(8,128)(2,1)S(1)}, bf16[32,4096]{1,0:T(8,128)(2,1)S(1)}, u32[]{:S(2)}, u32[]{:S(2)}) collective-permute-start(bf16[32,4096]{1,0:T(8,128)(2,1)S(1)} %reshape.212), channel_id=1, source_target_pairs={{0,96},{1,25},{8,104},{9,1},{16,112},{17,9},{24,120},{25,17},{32,0... | collective-permute-start | bytes 786440 | tf_op jit(solution)/shard_map/ppermute | solution.py:41
  81.0 5.2 %collective-permute-done.19 = bf16[32,4096]{1,0:T(8,128)(2,1)S(1)} collective-permute-done((bf16[32,4096]{1,0:T(8,128)(2,1)S(1)}, bf16[32,4096]{1,0:T(8,128)(2,1)S(1)}, u32[]{:S(2)}, u32[]{:S(2)}) %collective-permute-start.19) | collective-permute-done | bytes 262176 | tf_op jit(solution)/shard_map/ppermute | solution.py:41
  87.2 2.8 %collective-permute-done.17 = bf16[32,4096]{1,0:T(8,128)(2,1)S(1)} collective-permute-done((bf16[32,4096]{1,0:T(8,128)(2,1)S(1)}, bf16[32,4096]{1,0:T(8,128)(2,1)S(1)}, u32[]{:S(2)}, u32[]{:S(2)}) %collective-permute-start.17) | collective-permute-done | bytes 262176 | tf_op jit(solution)/shard_map/ppermute | solution.py:41
  90.1 1.3 collective-permute-start.21
  91.6 7.3 %load_weights.1 = (bf16[4096,896]{1,0:T(8,128)(2,1)S(1)}, bf16[4096,896]{1,0:T(8,128)(2,1)S(1)}, bf16[896,4096]{1,0:T(8,128)(2,1)S(1)}) custom-call(bf16[4096,896]{1,0:T(8,128)(2,1)} %bitcast.101, bf16[4096,896]{1,0:T(8,128)(2,1)} %bitcast.102, bf16[896,4096]{1,0:T(8,128)(2,1)} %bitcast.103, bf16[4,32,4096]{2,1,0:T(8,128)(2,1)S(1)} %pad_maximum_fusion.refs_3_), custom_call_target="tpu_custom_call" | custom-call | tf_op jit(solution)/shard_map/load_weights/pallas_call | solution.py:194
  98.9 3.5 %expert_rows.4.refs_4_ = bf16[128,4096]{1,0:T(8,128)(2,1)S(1)} custom-call(bf16[128,4096]{1,0:T(8,128)(2,1)S(1)} %bitcast.99, bf16[4096,896]{1,0:T(8,128)(2,1)S(1)} %get-tuple-element.24.refs_1_.refs_2_, bf16[4096,896]{1,0:T(8,128)(2,1)S(1)} %get-tuple-element.25.refs_2_.refs_3_, bf16[896,4096]{1,0:T(8,128)(2,1)S(1)} %get-tuple-element.26.refs_3_.refs_4_, ...), custom_call_target="tpu_custom_call" | custom-call | tf_op jit(solution)/shard_map/expert_rows/pallas_call | solution.py:136
  102.4 1.7 collective-permute-done.21.refs_0_
  104.1 2.4 %collective-permute-done.20.refs_0_ = bf16[128,4096]{1,0:T(8,128)(2,1)S(1)} collective-permute-done((bf16[128,4096]{1,0:T(8,128)(2,1)S(1)}, bf16[128,4096]{1,0:T(8,128)(2,1)S(1)}, u32[]{:S(2)}, u32[]{:S(2)}) %collective-permute-start.20) | collective-permute-done | bytes 1048608 | tf_op jit(solution)/shard_map/ppermute | solution.py:41
  106.6 1.2 collective-permute-start.23
  108.1 3.5 %expert_rows.5.refs_4_ = bf16[128,4096]{1,0:T(8,128)(2,1)S(1)} custom-call(bf16[128,4096]{1,0:T(8,128)(2,1)S(1)} %collective-permute-done.20.refs_0_, bf16[4096,896]{1,0:T(8,128)(2,1)S(1)} %get-tuple-element.24.refs_1_.refs_2_, bf16[4096,896]{1,0:T(8,128)(2,1)S(1)} %get-tuple-element.25.refs_2_.refs_3_, ...), custom_call_target="tpu_custom_call" | custom-call | tf_op jit(solution)/shard_map/expert_rows/pallas_call | solution.py:136
  111.6 3.5 %expert_rows.6.refs_5_ = bf16[128,4096]{1,0:T(8,128)(2,1)S(1)} custom-call(bf16[128,4096]{1,0:T(8,128)(2,1)S(1)} %collective-permute-done.21.refs_0_, bf16[4096,896]{1,0:T(8,128)(2,1)S(1)} %get-tuple-element.24.refs_1_.refs_2_, bf16[4096,896]{1,0:T(8,128)(2,1)S(1)} %get-tuple-element.25.refs_2_.refs_3_, ...), custom_call_target="tpu_custom_call" | custom-call | tf_op jit(solution)/shard_map/expert_rows/pallas_call | solution.py:136
  115.1 2.2 %collective-permute-done.22.refs_0_ = bf16[64,4096]{1,0:T(8,128)(2,1)S(1)} collective-permute-done((bf16[64,4096]{1,0:T(8,128)(2,1)S(1)}, bf16[64,4096]{1,0:T(8,128)(2,1)S(1)}, u32[]{:S(2)}, u32[]{:S(2)}) %collective-permute-start.22) | collective-permute-done | bytes 524320 | tf_op jit(solution)/shard_map/ppermute | solution.py:41
  117.3 3.5 %expert_rows.7 = (bf16[64,4096]{1,0:T(8,128)(2,1)S(1)}, bf16[64,4096]{1,0:T(8,128)(2,1)S(1)}) custom-call(bf16[64,4096]{1,0:T(8,128)(2,1)S(1)} %collective-permute-done.22.refs_0_, bf16[64,4096]{1,0:T(8,128)(2,1)S(1)} %collective-permute-done.23.refs_1_, bf16[4096,896]{1,0:T(8,128)(2,1)S(1)} %get-tuple-element.24.refs_1_.refs_2_, ...), custom_call_target="tpu_custom_call" | custom-call | tf_op jit(solution)/shard_map/expert_rows/pallas_call | solution.py:136
  120.9 2.7 %collective-permute-start.24 = (bf16[64,4096]{1,0:T(8,128)(2,1)S(1)}, bf16[64,4096]{1,0:T(8,128)(2,1)S(1)}, u32[]{:S(2)}, u32[]{:S(2)}) collective-permute-start(bf16[64,4096]{1,0:T(8,128)(2,1)S(1)} %get-tuple-element.30), channel_id=1, source_target_pairs={{0,24},{1,97},{8,0},{9,105},{16,8},{17,113},{24,16},{25,121},{32,5... | collective-permute-start | bytes 1572872 | tf_op jit(solution)/shard_map/ppermute | solution.py:41
  123.6 6.9 %collective-permute-done.26 = bf16[64,4096]{1,0:T(8,128)(2,1)S(1)} collective-permute-done((bf16[64,4096]{1,0:T(8,128)(2,1)S(1)}, bf16[64,4096]{1,0:T(8,128)(2,1)S(1)}, u32[]{:S(2)}, u32[]{:S(2)}) %collective-permute-start.26) | collective-permute-done | bytes 524320 | tf_op jit(solution)/shard_map/ppermute | solution.py:41
  130.9 3.0 %collective-permute-start.25 = (bf16[128,4096]{1,0:T(8,128)(2,1)S(1)}, bf16[128,4096]{1,0:T(8,128)(2,1)S(1)}, u32[]{:S(2)}, u32[]{:S(2)}) collective-permute-start(bf16[128,4096]{1,0:T(8,128)(2,1)S(1)} %pad_maximum_fusion.1), channel_id=1, source_target_pairs={{0,24},{1,97},{8,0},{9,105},{16,8},{17,113},{24,16},{25,121},{32,5... | collective-permute-start | bytes 3145736 | tf_op jit(solution)/shard_map/ppermute | solution.py:41
  133.9 12.0 %collective-permute-done.27 = bf16[128,4096]{1,0:T(8,128)(2,1)S(1)} collective-permute-done((bf16[128,4096]{1,0:T(8,128)(2,1)S(1)}, bf16[128,4096]{1,0:T(8,128)(2,1)S(1)}, u32[]{:S(2)}, u32[]{:S(2)}) %collective-permute-start.27) | collective-permute-done | bytes 1048608 | tf_op jit(solution)/shard_map/ppermute | solution.py:41
  148.6 4.8 %collective-permute-done.28 = bf16[32,4096]{1,0:T(8,128)(2,1)S(1)} collective-permute-done((bf16[32,4096]{1,0:T(8,128)(2,1)S(1)}, bf16[32,4096]{1,0:T(8,128)(2,1)S(1)}, u32[]{:S(2)}, u32[]{:S(2)}) %collective-permute-start.28) | collective-permute-done | bytes 262176 | tf_op jit(solution)/shard_map/ppermute | solution.py:41
  153.3 3.5 %collective-permute-done.30 = bf16[32,4096]{1,0:T(8,128)(2,1)S(1)} collective-permute-done((bf16[32,4096]{1,0:T(8,128)(2,1)S(1)}, bf16[32,4096]{1,0:T(8,128)(2,1)S(1)}, u32[]{:S(2)}, u32[]{:S(2)}) %collective-permute-start.30) | collective-permute-done | bytes 262176 | tf_op jit(solution)/shard_map/ppermute | solution.py:41
  158.7 1.6 collective-permute-done.31
  160.3 2.0 %collective-permute-done.32 = bf16[2,4,4096]{2,1,0:T(4,128)(2,1)S(1)} collective-permute-done((bf16[2,4,4096]{2,1,0:T(4,128)(2,1)S(1)}, bf16[2,4,4096]{2,1,0:T(4,128)(2,1)S(1)}, u32[]{:S(2)}, u32[]{:S(2)}) %collective-permute-start.32) | collective-permute-done | bytes 65568 | tf_op jit(solution)/shard_map/ppermute | solution.py:27
  163.5 14.1 %collective-permute-start.34 = (bf16[4,4,4096]{2,1,0:T(4,128)(2,1)S(1)}, bf16[4,4,4096]{2,1,0:T(4,128)(2,1)S(1)}, u32[]{:S(2)}, u32[]{:S(2)}) collective-permute-start(bf16[4,4,4096]{2,1,0:T(4,128)(2,1)S(1)} %get-tuple-element.43), channel_id=1, source_target_pairs={{0,1},{1,0},{2,3},{3,2},{4,5},{5,4},{6,7},{7,6},{8,9},{9,8},{10,11... | collective-permute-start | bytes 393224 | tf_op jit(solution)/shard_map/ppermute | solution.py:45
  (132 shorter events, 23.0 us)
Async XLA Ops:
  0.6 37.0 %copy-start = (bf16[64,64,128]{2,1,0:T(8,128)(2,1)S(1)}, bf16[64,64,128]{2,1,0:T(8,128)(2,1)}, u32[]{:S(2)}) copy-start(bf16[64,64,128]{2,1,0:T(8,128)(2,1)} %param.22) | copy-start | bytes 3145732
  3.4 15.9 %all-to-all-start = ((bf16[16,16,512]{2,1,0:T(8,128)(2,1)}), bf16[16,16,512]{2,1,0:T(8,128)(2,1)S(1)}, u32[]{:S(2)}, u32[]{:S(2)}) async-start(bf16[16,16,512]{2,1,0:T(8,128)(2,1)} %bitcast.3), calls=%async_computation | async-start | bytes 524288 | tf_op jit(solution)/shard_map/all_to_all | solution.py:245
  14.2 15.3 %copy-start.2 = (bf16[512,256]{1,0:T(8,128)(2,1)S(1)}, bf16[512,256]{1,0:T(8,128)(2,1)}, u32[]{:S(2)}) copy-start(bf16[512,256]{1,0:T(8,128)(2,1)} %refs_4_.1) | copy-start | bytes 786436
  24.4 12.3 %all-to-all-start.1 = ((bf16[16,16,640]{2,1,0:T(8,128)(2,1)}), bf16[16,16,640]{2,1,0:T(8,128)(2,1)S(1)}, u32[]{:S(2)}, u32[]{:S(2)}) async-start(bf16[16,16,640]{2,1,0:T(8,128)(2,1)} %bitcast.6), calls=%async_computation.1 | async-start | bytes 655360 | tf_op jit(solution)/shard_map/all_to_all | solution.py:254
  29.5 11.9 %collective-permute-start.5 = (bf16[512,256]{1,0:T(8,128)(2,1)S(1)}, bf16[512,256]{1,0:T(8,128)(2,1)S(1)}, u32[]{:S(2)}, u32[]{:S(2)}) collective-permute-start(bf16[512,256]{1,0:T(8,128)(2,1)S(1)} %copy-done.2), channel_id=1, source_target_pairs={{0,32},{32,64},{64,96},{96,0},{1,33},{33,65},{65,97},{97,1},{2,34}... | collective-permute-start | bytes 786440 | tf_op jit(solution)/shard_map/ppermute | solution.py:27
  30.9 15.2 %collective-permute-start.4 = (bf16[512,256]{1,0:T(8,128)(2,1)S(1)}, bf16[512,256]{1,0:T(8,128)(2,1)S(1)}, u32[]{:S(2)}, u32[]{:S(2)}) collective-permute-start(bf16[512,256]{1,0:T(8,128)(2,1)S(1)} %copy-done.2), channel_id=1, source_target_pairs={{0,64},{32,96},{64,0},{96,32},{1,65},{33,97},{65,1},{97,33},{2,66}... | collective-permute-start | bytes 786440 | tf_op jit(solution)/shard_map/ppermute | solution.py:27
  33.3 12.8 %collective-permute-start.3 = (bf16[512,256]{1,0:T(8,128)(2,1)S(1)}, bf16[512,256]{1,0:T(8,128)(2,1)S(1)}, u32[]{:S(2)}, u32[]{:S(2)}) collective-permute-start(bf16[512,256]{1,0:T(8,128)(2,1)S(1)} %copy-done.2), channel_id=1, source_target_pairs={{0,96},{32,0},{64,32},{96,64},{1,97},{33,1},{65,33},{97,65},{2,98}... | collective-permute-start | bytes 786440 | tf_op jit(solution)/shard_map/ppermute | solution.py:27
  37.0 5.6 %copy-start.5 = (s32[8,2]{0,1:T(2,128)S(1)}, s32[8,2]{0,1:T(2,128)}, u32[]{:S(2)}) copy-start(s32[8,2]{0,1:T(2,128)} %param.31) | copy-start | bytes 196
  38.1 26.2 %copy-start.4 = (bf16[8,4096]{1,0:T(8,128)(2,1)S(1)}, bf16[8,4096]{1,0:T(8,128)(2,1)}, u32[]{:S(2)}) copy-start(bf16[8,4096]{1,0:T(8,128)(2,1)} %param.29) | copy-start | bytes 196612
  38.2 26.3 %copy-start.3 = (f32[4096]{0:T(1024)S(1)}, f32[4096]{0:T(1024)}, u32[]{:S(2)}) copy-start(f32[4096]{0:T(1024)} %refs_4_.2) | copy-start | bytes 49156
  38.3 7.8 %collective-permute-start.2 = (bf16[2,32,512]{2,1,0:T(8,128)(2,1)S(1)}, bf16[2,32,512]{2,1,0:T(8,128)(2,1)S(1)}, u32[]{:S(2)}, u32[]{:S(2)}) collective-permute-start(bf16[2,32,512]{2,1,0:T(8,128)(2,1)S(1)} %fusion.19.refs_0_), channel_id=1, source_target_pairs={{0,24},{8,0},{16,8},{24,16},{1,25},{9,1},{17,9},{25,17},{2,26},{10... | collective-permute-start | bytes 196616 | tf_op jit(solution)/shard_map/ppermute | solution.py:27
  39.1 7.0 %collective-permute-start.1 = (bf16[2,32,512]{2,1,0:T(8,128)(2,1)S(1)}, bf16[2,32,512]{2,1,0:T(8,128)(2,1)S(1)}, u32[]{:S(2)}, u32[]{:S(2)}) collective-permute-start(bf16[2,32,512]{2,1,0:T(8,128)(2,1)S(1)} %fusion.19.refs_0_), channel_id=1, source_target_pairs={{0,16},{8,24},{16,0},{24,8},{1,17},{9,25},{17,1},{25,9},{2,18},{10... | collective-permute-start | bytes 196616 | tf_op jit(solution)/shard_map/ppermute | solution.py:27
  41.4 4.7 %collective-permute-start = (bf16[2,32,512]{2,1,0:T(8,128)(2,1)S(1)}, bf16[2,32,512]{2,1,0:T(8,128)(2,1)S(1)}, u32[]{:S(2)}, u32[]{:S(2)}) collective-permute-start(bf16[2,32,512]{2,1,0:T(8,128)(2,1)S(1)} %fusion.19.refs_0_), channel_id=1, source_target_pairs={{0,8},{8,16},{16,24},{24,0},{1,9},{9,17},{17,25},{25,1},{2,10},{10... | collective-permute-start | bytes 196616 | tf_op jit(solution)/shard_map/ppermute | solution.py:27
  46.6 5.2 %collective-permute-start.6 = (bf16[4,4,8,1024]{3,2,1,0:T(8,128)(2,1)S(1)}, bf16[4,4,8,1024]{3,2,1,0:T(8,128)(2,1)S(1)}, u32[]{:S(2)}, u32[]{:S(2)}) collective-permute-start(bf16[4,4,8,1024]{3,2,1,0:T(8,128)(2,1)S(1)} %get-tuple-element.20), channel_id=1, source_target_pairs={{0,1},{1,0},{2,3},{3,2},{4,5},{5,4},{6,7},{7,6},{8,9},{9,8},{10,11... | collective-permute-start | bytes 786440 | tf_op jit(solution)/shard_map/ppermute | solution.py:45
  51.8 4.5 %collective-permute-start.7 = (bf16[4,8,1024]{2,1,0:T(8,128)(2,1)S(1)}, bf16[4,8,1024]{2,1,0:T(8,128)(2,1)S(1)}, u32[]{:S(2)}, u32[]{:S(2)}) collective-permute-start(bf16[4,8,1024]{2,1,0:T(8,128)(2,1)S(1)} %get-tuple-element.54), channel_id=1, source_target_pairs={{0,2},{2,4},{4,6},{6,0},{1,3},{3,5},{5,7},{7,1},{8,10},{10,12},{12... | collective-permute-start | bytes 196616 | tf_op jit(solution)/shard_map/ppermute | solution.py:27
  53.2 3.2 %collective-permute-start.9 = (bf16[4,8,1024]{2,1,0:T(8,128)(2,1)S(1)}, bf16[4,8,1024]{2,1,0:T(8,128)(2,1)S(1)}, u32[]{:S(2)}, u32[]{:S(2)}) collective-permute-start(bf16[4,8,1024]{2,1,0:T(8,128)(2,1)S(1)} %get-tuple-element.55), channel_id=1, source_target_pairs={{0,6},{2,0},{4,2},{6,4},{1,7},{3,1},{5,3},{7,5},{8,14},{10,8},{12,... | collective-permute-start | bytes 196616 | tf_op jit(solution)/shard_map/ppermute | solution.py:27
  54.7 4.6 %collective-permute-start.8 = (bf16[4,8,1024]{2,1,0:T(8,128)(2,1)S(1)}, bf16[4,8,1024]{2,1,0:T(8,128)(2,1)S(1)}, u32[]{:S(2)}, u32[]{:S(2)}) collective-permute-start(bf16[4,8,1024]{2,1,0:T(8,128)(2,1)S(1)} %get-tuple-element.56), channel_id=1, source_target_pairs={{0,4},{2,6},{4,0},{6,2},{1,5},{3,7},{5,1},{7,3},{8,12},{10,14},{12... | collective-permute-start | bytes 196616 | tf_op jit(solution)/shard_map/ppermute | solution.py:27
  59.4 4.8 %collective-permute-start.12 = (bf16[8,1024]{1,0:T(8,128)(2,1)S(1)}, bf16[8,1024]{1,0:T(8,128)(2,1)S(1)}, u32[]{:S(2)}, u32[]{:S(2)}) collective-permute-start(bf16[8,1024]{1,0:T(8,128)(2,1)S(1)} %get-tuple-element.57), channel_id=1, source_target_pairs={{0,8},{8,16},{16,24},{24,0},{1,9},{9,17},{17,25},{25,1},{2,10},{10... | collective-permute-start | bytes 49160 | tf_op jit(solution)/shard_map/ppermute | solution.py:27
  59.5 4.7 %collective-permute-start.11 = (bf16[8,1024]{1,0:T(8,128)(2,1)S(1)}, bf16[8,1024]{1,0:T(8,128)(2,1)S(1)}, u32[]{:S(2)}, u32[]{:S(2)}) collective-permute-start(bf16[8,1024]{1,0:T(8,128)(2,1)S(1)} %get-tuple-element.58), channel_id=1, source_target_pairs={{0,16},{8,24},{16,0},{24,8},{1,17},{9,25},{17,1},{25,9},{2,18},{10... | collective-permute-start | bytes 49160 | tf_op jit(solution)/shard_map/ppermute | solution.py:27
  61.6 2.6 %collective-permute-start.10 = (bf16[8,1024]{1,0:T(8,128)(2,1)S(1)}, bf16[8,1024]{1,0:T(8,128)(2,1)S(1)}, u32[]{:S(2)}, u32[]{:S(2)}) collective-permute-start(bf16[8,1024]{1,0:T(8,128)(2,1)S(1)} %get-tuple-element.59), channel_id=1, source_target_pairs={{0,24},{8,0},{16,8},{24,16},{1,25},{9,1},{17,9},{25,17},{2,26},{10... | collective-permute-start | bytes 49160 | tf_op jit(solution)/shard_map/ppermute | solution.py:27
  65.0 4.7 %collective-permute-start.13 = (bf16[4,4,4096]{2,1,0:T(4,128)(2,1)S(1)}, bf16[4,4,4096]{2,1,0:T(4,128)(2,1)S(1)}, u32[]{:S(2)}, u32[]{:S(2)}) collective-permute-start(bf16[4,4,4096]{2,1,0:T(4,128)(2,1)S(1)} %get-tuple-element.53), channel_id=1, source_target_pairs={{0,1},{1,0},{2,3},{3,2},{4,5},{5,4},{6,7},{7,6},{8,9},{9,8},{10,11... | collective-permute-start | bytes 393224 | tf_op jit(solution)/shard_map/ppermute | solution.py:45
  70.0 4.4 %collective-permute-start.14 = (bf16[2,4,4096]{2,1,0:T(4,128)(2,1)S(1)}, bf16[2,4,4096]{2,1,0:T(4,128)(2,1)S(1)}, u32[]{:S(2)}, u32[]{:S(2)}) collective-permute-start(bf16[2,4,4096]{2,1,0:T(4,128)(2,1)S(1)} %get-tuple-element.49), channel_id=1, source_target_pairs={{0,2},{2,4},{4,6},{6,0},{1,3},{3,5},{5,7},{7,1},{8,10},{10,12},{12... | collective-permute-start | bytes 196616 | tf_op jit(solution)/shard_map/ppermute | solution.py:27
  70.1 4.2 %collective-permute-start.16 = (bf16[2,4,4096]{2,1,0:T(4,128)(2,1)S(1)}, bf16[2,4,4096]{2,1,0:T(4,128)(2,1)S(1)}, u32[]{:S(2)}, u32[]{:S(2)}) collective-permute-start(bf16[2,4,4096]{2,1,0:T(4,128)(2,1)S(1)} %get-tuple-element.50), channel_id=1, source_target_pairs={{0,6},{2,0},{4,2},{6,4},{1,7},{3,1},{5,3},{7,5},{8,14},{10,8},{12,... | collective-permute-start | bytes 196616 | tf_op jit(solution)/shard_map/ppermute | solution.py:27
  72.7 4.6 %collective-permute-start.15 = (bf16[2,4,4096]{2,1,0:T(4,128)(2,1)S(1)}, bf16[2,4,4096]{2,1,0:T(4,128)(2,1)S(1)}, u32[]{:S(2)}, u32[]{:S(2)}) collective-permute-start(bf16[2,4,4096]{2,1,0:T(4,128)(2,1)S(1)} %get-tuple-element.51), channel_id=1, source_target_pairs={{0,4},{2,6},{4,0},{6,2},{1,5},{3,7},{5,1},{7,3},{8,12},{10,14},{12... | collective-permute-start | bytes 196616 | tf_op jit(solution)/shard_map/ppermute | solution.py:27
  77.6 8.6 %collective-permute-start.19 = (bf16[32,4096]{1,0:T(8,128)(2,1)S(1)}, bf16[32,4096]{1,0:T(8,128)(2,1)S(1)}, u32[]{:S(2)}, u32[]{:S(2)}) collective-permute-start(bf16[32,4096]{1,0:T(8,128)(2,1)S(1)} %reshape.212), channel_id=1, source_target_pairs={{0,96},{1,25},{8,104},{9,1},{16,112},{17,9},{24,120},{25,17},{32,0... | collective-permute-start | bytes 786440 | tf_op jit(solution)/shard_map/ppermute | solution.py:41
  80.1 7.1 %collective-permute-start.18 = (bf16[32,4096]{1,0:T(8,128)(2,1)S(1)}, bf16[32,4096]{1,0:T(8,128)(2,1)S(1)}, u32[]{:S(2)}, u32[]{:S(2)}) collective-permute-start(bf16[32,4096]{1,0:T(8,128)(2,1)S(1)} %reshape.212), channel_id=1, source_target_pairs={{0,64},{1,17},{8,72},{9,25},{16,80},{17,1},{24,88},{25,9},{32,96},... | collective-permute-start | bytes 786440 | tf_op jit(solution)/shard_map/ppermute | solution.py:41
  80.6 9.3 %collective-permute-start.17 = (bf16[32,4096]{1,0:T(8,128)(2,1)S(1)}, bf16[32,4096]{1,0:T(8,128)(2,1)S(1)}, u32[]{:S(2)}, u32[]{:S(2)}) collective-permute-start(bf16[32,4096]{1,0:T(8,128)(2,1)S(1)} %reshape.212), channel_id=1, source_target_pairs={{0,32},{1,9},{8,40},{9,17},{16,48},{17,25},{24,56},{25,1},{32,64},... | collective-permute-start | bytes 786440 | tf_op jit(solution)/shard_map/ppermute | solution.py:41
  90.1 14.0 %collective-permute-start.21 = (bf16[128,4096]{1,0:T(8,128)(2,1)S(1)}, bf16[128,4096]{1,0:T(8,128)(2,1)S(1)}, u32[]{:S(2)}, u32[]{:S(2)}) collective-permute-start(bf16[128,4096]{1,0:T(8,128)(2,1)S(1)} %bitcast.97), channel_id=1, source_target_pairs={{0,24},{1,97},{8,0},{9,105},{16,8},{17,113},{24,16},{25,121},{32,5... | collective-permute-start | bytes 3145736 | tf_op jit(solution)/shard_map/ppermute | solution.py:41
  91.3 15.2 %collective-permute-start.20 = (bf16[128,4096]{1,0:T(8,128)(2,1)S(1)}, bf16[128,4096]{1,0:T(8,128)(2,1)S(1)}, u32[]{:S(2)}, u32[]{:S(2)}) collective-permute-start(bf16[128,4096]{1,0:T(8,128)(2,1)S(1)} %bitcast.98), channel_id=1, source_target_pairs={{0,8},{1,33},{8,16},{9,41},{16,24},{17,49},{24,0},{25,57},{32,40},... | collective-permute-start | bytes 3145736 | tf_op jit(solution)/shard_map/ppermute | solution.py:41
  106.6 8.6 %collective-permute-start.23 = (bf16[64,4096]{1,0:T(8,128)(2,1)S(1)}, bf16[64,4096]{1,0:T(8,128)(2,1)S(1)}, u32[]{:S(2)}, u32[]{:S(2)}) collective-permute-start(bf16[64,4096]{1,0:T(8,128)(2,1)S(1)} %slice.124), channel_id=1, source_target_pairs={{0,24},{1,97},{8,0},{9,105},{16,8},{17,113},{24,16},{25,121},{32,5... | collective-permute-start | bytes 1572872 | tf_op jit(solution)/shard_map/ppermute | solution.py:41
  107.8 9.5 %collective-permute-start.22 = (bf16[64,4096]{1,0:T(8,128)(2,1)S(1)}, bf16[64,4096]{1,0:T(8,128)(2,1)S(1)}, u32[]{:S(2)}, u32[]{:S(2)}) collective-permute-start(bf16[64,4096]{1,0:T(8,128)(2,1)S(1)} %slice.123), channel_id=1, source_target_pairs={{0,8},{1,33},{8,16},{9,41},{16,24},{17,49},{24,0},{25,57},{32,40},... | collective-permute-start | bytes 1572872 | tf_op jit(solution)/shard_map/ppermute | solution.py:41
  120.8 9.6 %collective-permute-start.26 = (bf16[64,4096]{1,0:T(8,128)(2,1)S(1)}, bf16[64,4096]{1,0:T(8,128)(2,1)S(1)}, u32[]{:S(2)}, u32[]{:S(2)}) collective-permute-start(bf16[64,4096]{1,0:T(8,128)(2,1)S(1)} %get-tuple-element.31), channel_id=1, source_target_pairs={{0,8},{1,33},{8,16},{9,41},{16,24},{17,49},{24,0},{25,57},{32,40},... | collective-permute-start | bytes 1572872 | tf_op jit(solution)/shard_map/ppermute | solution.py:41
  120.9 9.8 %collective-permute-start.24 = (bf16[64,4096]{1,0:T(8,128)(2,1)S(1)}, bf16[64,4096]{1,0:T(8,128)(2,1)S(1)}, u32[]{:S(2)}, u32[]{:S(2)}) collective-permute-start(bf16[64,4096]{1,0:T(8,128)(2,1)S(1)} %get-tuple-element.30), channel_id=1, source_target_pairs={{0,24},{1,97},{8,0},{9,105},{16,8},{17,113},{24,16},{25,121},{32,5... | collective-permute-start | bytes 1572872 | tf_op jit(solution)/shard_map/ppermute | solution.py:41
  130.6 15.2 %collective-permute-start.27 = (bf16[128,4096]{1,0:T(8,128)(2,1)S(1)}, bf16[128,4096]{1,0:T(8,128)(2,1)S(1)}, u32[]{:S(2)}, u32[]{:S(2)}) collective-permute-start(bf16[128,4096]{1,0:T(8,128)(2,1)S(1)} %pad_maximum_fusion.2), channel_id=1, source_target_pairs={{0,8},{1,33},{8,16},{9,41},{16,24},{17,49},{24,0},{25,57},{32,40},... | collective-permute-start | bytes 3145736 | tf_op jit(solution)/shard_map/ppermute | solution.py:41
  130.9 14.9 %collective-permute-start.25 = (bf16[128,4096]{1,0:T(8,128)(2,1)S(1)}, bf16[128,4096]{1,0:T(8,128)(2,1)S(1)}, u32[]{:S(2)}, u32[]{:S(2)}) collective-permute-start(bf16[128,4096]{1,0:T(8,128)(2,1)S(1)} %pad_maximum_fusion.1), channel_id=1, source_target_pairs={{0,24},{1,97},{8,0},{9,105},{16,8},{17,113},{24,16},{25,121},{32,5... | collective-permute-start | bytes 3145736 | tf_op jit(solution)/shard_map/ppermute | solution.py:41
  146.4 31.3 %copy-start.6 = (f32[8,2]{0,1:T(2,128)S(1)}, f32[8,2]{0,1:T(2,128)}, u32[]{:S(2)}) copy-start(f32[8,2]{0,1:T(2,128)} %param.32) | copy-start | bytes 196
  146.4 6.9 %collective-permute-start.28 = (bf16[32,4096]{1,0:T(8,128)(2,1)S(1)}, bf16[32,4096]{1,0:T(8,128)(2,1)S(1)}, u32[]{:S(2)}, u32[]{:S(2)}) collective-permute-start(bf16[32,4096]{1,0:T(8,128)(2,1)S(1)} %get-tuple-element.35), channel_id=1, source_target_pairs={{0,96},{1,25},{8,104},{9,1},{16,112},{17,9},{24,120},{25,17},{32,0... | collective-permute-start | bytes 786440 | tf_op jit(solution)/shard_map/ppermute | solution.py:41
  146.8 10.0 %collective-permute-start.30 = (bf16[32,4096]{1,0:T(8,128)(2,1)S(1)}, bf16[32,4096]{1,0:T(8,128)(2,1)S(1)}, u32[]{:S(2)}, u32[]{:S(2)}) collective-permute-start(bf16[32,4096]{1,0:T(8,128)(2,1)S(1)} %get-tuple-element.36), channel_id=1, source_target_pairs={{0,32},{1,9},{8,40},{9,17},{16,48},{17,25},{24,56},{25,1},{32,64},... | collective-permute-start | bytes 786440 | tf_op jit(solution)/shard_map/ppermute | solution.py:41
  147.9 8.9 %collective-permute-start.29 = (bf16[32,4096]{1,0:T(8,128)(2,1)S(1)}, bf16[32,4096]{1,0:T(8,128)(2,1)S(1)}, u32[]{:S(2)}, u32[]{:S(2)}) collective-permute-start(bf16[32,4096]{1,0:T(8,128)(2,1)S(1)} %get-tuple-element.37), channel_id=1, source_target_pairs={{0,64},{1,17},{8,72},{9,25},{16,80},{17,1},{24,88},{25,9},{32,96},... | collective-permute-start | bytes 786440 | tf_op jit(solution)/shard_map/ppermute | solution.py:41
  156.8 22.9 %copy-start.1 = (bf16[64,64,128]{2,1,0:T(8,128)(2,1)S(1)}, bf16[64,64,128]{2,1,0:T(8,128)(2,1)}, u32[]{:S(2)}) copy-start(bf16[64,64,128]{2,1,0:T(8,128)(2,1)} %param.22) | copy-start | bytes 3145732
  157.1 3.2 %collective-permute-start.31 = (bf16[2,4,4096]{2,1,0:T(4,128)(2,1)S(1)}, bf16[2,4,4096]{2,1,0:T(4,128)(2,1)S(1)}, u32[]{:S(2)}, u32[]{:S(2)}) collective-permute-start(bf16[2,4,4096]{2,1,0:T(4,128)(2,1)S(1)} %squeeze.60), channel_id=1, source_target_pairs={{0,6},{2,0},{4,2},{6,4},{1,7},{3,1},{5,3},{7,5},{8,14},{10,8},{12,... | collective-permute-start | bytes 196616 | tf_op jit(solution)/shard_map/ppermute | solution.py:27
  157.6 4.6 %collective-permute-start.32 = (bf16[2,4,4096]{2,1,0:T(4,128)(2,1)S(1)}, bf16[2,4,4096]{2,1,0:T(4,128)(2,1)S(1)}, u32[]{:S(2)}, u32[]{:S(2)}) collective-permute-start(bf16[2,4,4096]{2,1,0:T(4,128)(2,1)S(1)} %squeeze.61), channel_id=1, source_target_pairs={{0,4},{2,6},{4,0},{6,2},{1,5},{3,7},{5,1},{7,3},{8,12},{10,14},{12... | collective-permute-start | bytes 196616 | tf_op jit(solution)/shard_map/ppermute | solution.py:27
  157.9 5.4 %collective-permute-start.33 = (bf16[2,4,4096]{2,1,0:T(4,128)(2,1)S(1)}, bf16[2,4,4096]{2,1,0:T(4,128)(2,1)S(1)}, u32[]{:S(2)}, u32[]{:S(2)}) collective-permute-start(bf16[2,4,4096]{2,1,0:T(4,128)(2,1)S(1)} %squeeze.62), channel_id=1, source_target_pairs={{0,2},{2,4},{4,6},{6,0},{1,3},{3,5},{5,7},{7,1},{8,10},{10,12},{12... | collective-permute-start | bytes 196616 | tf_op jit(solution)/shard_map/ppermute | solution.py:27
  163.5 15.1 %collective-permute-start.34 = (bf16[4,4,4096]{2,1,0:T(4,128)(2,1)S(1)}, bf16[4,4,4096]{2,1,0:T(4,128)(2,1)S(1)}, u32[]{:S(2)}, u32[]{:S(2)}) collective-permute-start(bf16[4,4,4096]{2,1,0:T(4,128)(2,1)S(1)} %get-tuple-element.43), channel_id=1, source_target_pairs={{0,1},{1,0},{2,3},{3,2},{4,5},{5,4},{6,7},{7,6},{8,9},{9,8},{10,11... | collective-permute-start | bytes 393224 | tf_op jit(solution)/shard_map/ppermute | solution.py:45
where the time goes:
time: 180 us
  starting transfers between devices  70 us (39%)
  waiting for transfers between devices  66.2 us (37%)
  Pallas kernels  26.8 us (15%)
  matrix products  6.48 us (4%)
  other arithmetic  5.43 us (3%)
  local copies, waits for them, and re-layouts  3.57 us (2%)
    ppermute x14, waiting for transfers between devices, turn(): return lax.ppermute(block, ('x', 'z', 'k'), pairs)  42.3 us
    ppermute x3, starting transfers between devices, swap(): return lax.ppermute(block, 'k', [(0, 1), (1, 0)])  21.9 us
    ppermute x18, starting transfers between devices, push(): lax.ppermute(block, axis, [(i, (i + distance) % RING) for i in range(RING)])  20.7 us
    ppermute x18, waiting for transfers between devices, push(): lax.ppermute(block, axis, [(i, (i + distance) % RING) for i in range(RING)])  17.6 us
    ppermute x14, starting transfers between devices, turn(): return lax.ppermute(block, ('x', 'z', 'k'), pairs)  14.4 us
    pallas_call x4, Pallas kernels, apply_expert(): pl.pallas_call(lambda *refs: expert_kernel(count, *refs), in_specs=[local...  14 us
    all_to_all x1, starting transfers between devices, on_device(): lax.all_to_all(sent, CACHE, split_axis=0, concat_axis=0, tiled=True)  8.43 us
    pallas_call x1, Pallas kernels, loaded(): pl.pallas_call(lambda *refs: load_kernel(count, *refs), in_specs=[far] *...  7.28 us
  transfers between devices with their start and end apart: 37, of which 24 were waited for; matrix products, arithmetic and copies ran while one was open for 5% of the time, Pallas kernels for 10%

commit v1 on v0

--- a/solution.py
+++ b/solution.py
@@ -66,28 +66,81 @@
     return (first, second, rest - second)
 
 
+def dispatch_kernel(group_ids, slot_group, query, sent, placing, groups, held, queries, sems):
+    copies = [
+        pltpu.make_async_copy(group_ids, groups, sems.at[0]),
+        pltpu.make_async_copy(slot_group, held, sems.at[1]),
+        pltpu.make_async_copy(query, queries, sems.at[2]),
+    ]
+    for copy in copies:
+        copy.start()
+    count, slots = groups.shape[1], held.shape[1]
+    column = lax.broadcasted_iota(jnp.int32, (slots, slots), 1)
+    same = lax.broadcasted_iota(jnp.int32, (slots, slots), 0) == column
+    earlier = lax.broadcasted_iota(jnp.int32, (count, count), 0)
+    earlier = (earlier < lax.broadcasted_iota(jnp.int32, (count, count), 1)).astype(F32)
+    number = lax.broadcasted_iota(jnp.int32, (slots, count), 0).astype(F32) * MOSTG
+    places = lax.broadcasted_iota(jnp.int32, (slots * MOSTG, count), 0).astype(F32)
+    copies[0].wait()
+    copies[1].wait()
+    upright = jnp.sum(jnp.where(same, held[...].astype(F32), 0.0), axis=1, keepdims=True)
+    match = (upright == groups[...].astype(F32)).astype(F32)
+    before = jnp.dot(match, earlier, preferred_element_type=F32)
+    position = jnp.sum(match * (number + before), axis=0, keepdims=True)
+    chosen = jnp.where(places == position, 1.0, 0.0).astype(BF16)
+    placing[...] = chosen
+    copies[2].wait()
+    sent[...] = jnp.dot(chosen, queries[...], preferred_element_type=F32).astype(BF16)
+
+
+def dispatched(group_ids, slot_group, query):
+    far = pl.BlockSpec(memory_space=pl.ANY)
+    local = pl.BlockSpec(memory_space=pltpu.VMEM)
+    count, slots = group_ids.shape[0], slot_group.shape[0]
+    return pl.pallas_call(
+        dispatch_kernel,
+        in_specs=[far] * 3,
+        out_specs=[local] * 2,
+        out_shape=[
+            jax.ShapeDtypeStruct((slots * MOSTG, query.shape[1]), BF16),
+            jax.ShapeDtypeStruct((slots * MOSTG, count), BF16),
+        ],
+        scratch_shapes=[
+            pltpu.VMEM((1, count), jnp.int32),
+            pltpu.VMEM((1, slots), jnp.int32),
+            pltpu.VMEM(query.shape, BF16),
+            pltpu.SemaphoreType.DMA((3,)),
+        ],
+        compiler_params=pltpu.CompilerParams(vmem_limit_bytes=16 * 1024 * 1024),
+        name="place_queries",
+    )(
+        *[
+            pltpu.with_memory_space_constraint(array, pltpu.HBM)
+            for array in (group_ids.reshape(1, count), slot_group.reshape(1, slots), query)
+        ]
+    )
+
+
 def prefix_kernel(heads, width, scale, received, keys, values, out):
     rows = received[...].astype(F32).reshape(-1, heads * width).astype(BF16)
     count = rows.shape[0]
-    queries = jnp.concatenate([rows[:, h * width : (h + 1) * width] for h in range(heads)], axis=0)
-    scores = lax.dot_general(
-        queries, keys[0], (((1,), (1,)), ((), ())), preferred_element_type=F32
-    )
-    scores = scores * scale
-    top = jnp.max(scores, axis=-1, keepdims=True)
-    expo = jnp.exp(scores - top)
-    total = jnp.sum(expo, axis=-1, keepdims=True)
-    summed = jnp.dot(expo.astype(BF16), values[0], preferred_element_type=F32)
-    outputs = summed / total
-    parts = in_pieces(top + jnp.log(total))
     lane = lax.broadcasted_iota(jnp.int32, (count, width), 1)
     packed = jnp.zeros((count, width), F32)
-    for p, part in enumerate(parts):
-        for h in range(heads):
-            packed = jnp.where(lane == p * heads + h, part[h * count : (h + 1) * count], packed)
     for h in range(heads):
-        block = outputs[h * count : (h + 1) * count].reshape(-1, 1, MOSTG, width)
+        scores = lax.dot_general(
+            rows[:, h * width : (h + 1) * width],
+            keys[0],
+            (((1,), (1,)), ((), ())),
+            preferred_element_type=F32,
+        )
+        top = jnp.max(scores, axis=-1, keepdims=True)
+        expo = jnp.exp2((scores - top) * (scale * math.log2(math.e)))
+        total = jnp.sum(expo, axis=-1, keepdims=True)
+        summed = jnp.dot(expo.astype(BF16), values[0], preferred_element_type=F32)
+        block = (summed / total).reshape(-1, 1, MOSTG, width)
         out[:, :, :, h * width : (h + 1) * width] = block.astype(BF16)
+        for p, part in enumerate(in_pieces(top * scale + jnp.log(total))):
+            packed = jnp.where(lane == p * heads + h, part, packed)
     out[:, :, :, heads * width :] = packed.reshape(-1, 1, MOSTG, width).astype(BF16)
 
 
@@ -232,16 +285,7 @@
     experts = 2 * RING
     tokens = hidden_in.shape[0]
 
-    slot_count = slot_group.shape[0]
-    matches = group_ids[:, 0][:, None] == slot_group[None, :]
-    slot = jnp.sum(jnp.where(matches, jnp.arange(slot_count, dtype=jnp.int32)[None, :], 0), axis=1)
-    order = jnp.arange(requests, dtype=jnp.int32)
-    earlier = order[None, :] < order[:, None]
-    rank = jnp.sum((slot[:, None] == slot[None, :]) & earlier, axis=1)
-    position = slot * MOSTG + rank
-    places = jnp.arange(slot_count * MOSTG, dtype=jnp.int32)
-    placing = (places[:, None] == position[None, :]).astype(BF16)
-    sent = jnp.dot(placing, query, preferred_element_type=F32).astype(BF16)
+    sent, placing = dispatched(group_ids, slot_group, query)
     received = lax.all_to_all(sent, CACHE, split_axis=0, concat_axis=0, tiled=True)
 
     queries = query.reshape(requests, heads, head_dim)

time: 180 us -> 179 us (level)
  Pallas kernels: 26.8 us -> 28.7 us
    pallas_call x0 -> x1, Pallas kernels: none -> 1.94 us  [dispatched(): pl.pallas_call(dispatch_kernel, in_specs=[far] * 3, out_specs=[local] * 2...]
where the time goes in v1:
time: 179 us
  starting transfers between devices  69.8 us (39%)
  waiting for transfers between devices  66.4 us (37%)
  Pallas kernels  28.7 us (16%)
  matrix products  4.71 us (3%)
  other arithmetic  4.39 us (2%)
  local copies, waits for them, and re-layouts  3.58 us (2%)
    ppermute x14, waiting for transfers between devices, turn(): return lax.ppermute(block, ('x', 'z', 'k'), pairs)  42.4 us
    ppermute x3, starting transfers between devices, swap(): return lax.ppermute(block, 'k', [(0, 1), (1, 0)])  21.8 us
    ppermute x18, starting transfers between devices, push(): lax.ppermute(block, axis, [(i, (i + distance) % RING) for i in range(RING)])  20.8 us
    ppermute x18, waiting for transfers between devices, push(): lax.ppermute(block, axis, [(i, (i + distance) % RING) for i in range(RING)])  17.6 us
    ppermute x14, starting transfers between devices, turn(): return lax.ppermute(block, ('x', 'z', 'k'), pairs)  14.2 us
    pallas_call x4, Pallas kernels, apply_expert(): pl.pallas_call(lambda *refs: expert_kernel(count, *refs), in_specs=[local...  14 us
    all_to_all x1, starting transfers between devices, on_device(): lax.all_to_all(sent, CACHE, split_axis=0, concat_axis=0, tiled=True)  8.44 us
    pallas_call x1, Pallas kernels, loaded(): pl.pallas_call(lambda *refs: load_kernel(count, *refs), in_specs=[far] *...  7.28 us
  transfers between devices with their start and end apart: 37, of which 24 were waited for; matrix products, arithmetic and copies ran while one was open for 5% of the time, Pallas kernels for 10%

profile of v1, /device:TPU:1, one launch (start us, length us, event | category | flops | bytes accessed | tf_op | source)
XLA Modules:
  0.0 178.8 jit_solution(10202272988806673834)
XLA Ops:
  0.6 1.9 %place_queries.1 = (bf16[256,512]{1,0:T(8,128)(2,1)}, bf16[256,64]{1,0:T(8,128)(2,1)S(1)}) custom-call(s32[1,64]{1,0:T(1,128)} %bitcast.132, s32[1,32]{1,0:T(1,128)} %bitcast.133, bf16[64,512]{1,0:T(8,128)(2,1)} %query.1), custom_call_target="tpu_custom_call" | custom-call | tf_op jit(solution)/shard_map/place_queries/pallas_call | solution.py:100
  2.6 8.4 %all-to-all-start = ((bf16[16,16,512]{2,1,0:T(8,128)(2,1)}), bf16[16,16,512]{2,1,0:T(8,128)(2,1)S(1)}, u32[]{:S(2)}, u32[]{:S(2)}) async-start(bf16[16,16,512]{2,1,0:T(8,128)(2,1)} %bitcast.4), calls=%async_computation | async-start | bytes 524288 | tf_op jit(solution)/shard_map/all_to_all | solution.py:289
  14.4 2.0 %fusion.47 = (f32[64,4]{1,0:T(8,128)S(1)}, f32[64,4,64]{2,1,0:T(4,128)S(1)}) fusion(bf16[64,4,128]{2,1,0:T(4,128)(2,1)S(1)} %reshape.201, bf16[64,64,128]{2,1,0:T(8,128)(2,1)} %param.21, pred[64,64]{1,0:T(8,128)(4,1)S(1)} %iota_compare_fusion), kind=kOutput, calls=%fused_computation.128 | convolution fusion | flops 4243200 | bytes 1184768 | tf_op jit(solution)/shard_map/rhd,rpd->rhp/dot_general | solution.py:49
  16.5 2.0 %all-to-all-done = bf16[16,16,512]{2,1,0:T(8,128)(2,1)S(1)} async-done(((bf16[16,16,512]{2,1,0:T(8,128)(2,1)}), bf16[16,16,512]{2,1,0:T(8,128)(2,1)S(1)}, u32[]{:S(2)}, u32[]{:S(2)}) %all-to-all-start) | async-done | bytes 262176 | tf_op jit(solution)/shard_map/all_to_all | solution.py:289
  18.5 5.0 %prefix_attention.1 = bf16[16,2,8,640]{3,2,1,0:T(8,128)(2,1)} custom-call(bf16[16,2,8,512]{3,2,1,0:T(8,128)(2,1)S(1)} %bitcast.101, bf16[2,1024,128]{2,1,0:T(8,128)(2,1)} %refs_1_.1, bf16[2,1024,128]{2,1,0:T(8,128)(2,1)} %refs_2_.1), custom_call_target="tpu_custom_call" | custom-call | tf_op jit(solution)/shard_map/prefix_attention/pallas_call | solution.py:150
  23.5 4.6 %all-to-all-start.1 = ((bf16[16,16,640]{2,1,0:T(8,128)(2,1)}), bf16[16,16,640]{2,1,0:T(8,128)(2,1)S(1)}, u32[]{:S(2)}, u32[]{:S(2)}) async-start(bf16[16,16,640]{2,1,0:T(8,128)(2,1)} %bitcast.7), calls=%async_computation.1 | async-start | bytes 655360 | tf_op jit(solution)/shard_map/all_to_all | solution.py:298
  28.6 1.4 collective-permute-start.5
  29.9 2.4 %collective-permute-start.4 = (bf16[512,256]{1,0:T(8,128)(2,1)S(1)}, bf16[512,256]{1,0:T(8,128)(2,1)S(1)}, u32[]{:S(2)}, u32[]{:S(2)}) collective-permute-start(bf16[512,256]{1,0:T(8,128)(2,1)S(1)} %copy-done.2), channel_id=1, source_target_pairs={{0,64},{32,96},{64,0},{96,32},{1,65},{33,97},{65,1},{97,33},{2,66}... | collective-permute-start | bytes 786440 | tf_op jit(solution)/shard_map/ppermute | solution.py:27
  32.3 1.2 collective-permute-start.3
  33.5 2.3 %all-to-all-done.1 = bf16[16,16,640]{2,1,0:T(8,128)(2,1)S(1)} async-done(((bf16[16,16,640]{2,1,0:T(8,128)(2,1)}), bf16[16,16,640]{2,1,0:T(8,128)(2,1)S(1)}, u32[]{:S(2)}, u32[]{:S(2)}) %all-to-all-start.1) | async-done | bytes 327712 | tf_op jit(solution)/shard_map/all_to_all | solution.py:298
  38.1 1.2 collective-permute-start.1
  39.3 1.2 collective-permute-done.5.refs_7_
  40.5 1.2 collective-permute-start
  41.8 3.3 %collective-permute-done.4.refs_6_ = bf16[512,256]{1,0:T(8,128)(2,1)S(1)} collective-permute-done((bf16[512,256]{1,0:T(8,128)(2,1)S(1)}, bf16[512,256]{1,0:T(8,128)(2,1)S(1)}, u32[]{:S(2)}, u32[]{:S(2)}) %collective-permute-start.4) | collective-permute-done | bytes 262176 | tf_op jit(solution)/shard_map/ppermute | solution.py:27
  45.7 4.0 %collective-permute-start.6 = (bf16[4,4,8,1024]{3,2,1,0:T(8,128)(2,1)S(1)}, bf16[4,4,8,1024]{3,2,1,0:T(8,128)(2,1)S(1)}, u32[]{:S(2)}, u32[]{:S(2)}) collective-permute-start(bf16[4,4,8,1024]{3,2,1,0:T(8,128)(2,1)S(1)} %get-tuple-element.24), channel_id=1, source_target_pairs={{0,1},{1,0},{2,3},{3,2},{4,5},{5,4},{6,7},{7,6},{8,9},{9,8},{10,11... | collective-permute-start | bytes 786440 | tf_op jit(solution)/shard_map/ppermute | solution.py:45
  50.9 1.4 collective-permute-start.7
  52.2 1.5 collective-permute-start.9
  53.7 1.6 collective-permute-start.8
  55.4 3.0 %collective-permute-done.8 = bf16[4,8,1024]{2,1,0:T(8,128)(2,1)S(1)} collective-permute-done((bf16[4,8,1024]{2,1,0:T(8,128)(2,1)S(1)}, bf16[4,8,1024]{2,1,0:T(8,128)(2,1)S(1)}, u32[]{:S(2)}, u32[]{:S(2)}) %collective-permute-start.8) | collective-permute-done | bytes 65568 | tf_op jit(solution)/shard_map/ppermute | solution.py:27
  58.5 2.1 %collective-permute-start.11 = (bf16[8,1024]{1,0:T(8,128)(2,1)S(1)}, bf16[8,1024]{1,0:T(8,128)(2,1)S(1)}, u32[]{:S(2)}, u32[]{:S(2)}) collective-permute-start(bf16[8,1024]{1,0:T(8,128)(2,1)S(1)} %get-tuple-element.62), channel_id=1, source_target_pairs={{0,16},{8,24},{16,0},{24,8},{1,17},{9,25},{17,1},{25,9},{2,18},{10... | collective-permute-start | bytes 49160 | tf_op jit(solution)/shard_map/ppermute | solution.py:27
  60.7 1.2 collective-permute-start.10
  61.8 1.4 collective-permute-done.10
  64.1 3.7 %collective-permute-start.13 = (bf16[4,4,4096]{2,1,0:T(4,128)(2,1)S(1)}, bf16[4,4,4096]{2,1,0:T(4,128)(2,1)S(1)}, u32[]{:S(2)}, u32[]{:S(2)}) collective-permute-start(bf16[4,4,4096]{2,1,0:T(4,128)(2,1)S(1)} %get-tuple-element.57), channel_id=1, source_target_pairs={{0,1},{1,0},{2,3},{3,2},{4,5},{5,4},{6,7},{7,6},{8,9},{9,8},{10,11... | collective-permute-start | bytes 393224 | tf_op jit(solution)/shard_map/ppermute | solution.py:45
  69.2 2.6 %collective-permute-start.16 = (bf16[2,4,4096]{2,1,0:T(4,128)(2,1)S(1)}, bf16[2,4,4096]{2,1,0:T(4,128)(2,1)S(1)}, u32[]{:S(2)}, u32[]{:S(2)}) collective-permute-start(bf16[2,4,4096]{2,1,0:T(4,128)(2,1)S(1)} %get-tuple-element.54), channel_id=1, source_target_pairs={{0,6},{2,0},{4,2},{6,4},{1,7},{3,1},{5,3},{7,5},{8,14},{10,8},{12,... | collective-permute-start | bytes 196616 | tf_op jit(solution)/shard_map/ppermute | solution.py:27
  72.3 1.2 collective-permute-done.14
  73.4 3.0 %collective-permute-done.15 = bf16[2,4,4096]{2,1,0:T(4,128)(2,1)S(1)} collective-permute-done((bf16[2,4,4096]{2,1,0:T(4,128)(2,1)S(1)}, bf16[2,4,4096]{2,1,0:T(4,128)(2,1)S(1)}, u32[]{:S(2)}, u32[]{:S(2)}) %collective-permute-start.15) | collective-permute-done | bytes 65568 | tf_op jit(solution)/shard_map/ppermute | solution.py:27
  76.7 2.5 %collective-permute-start.19 = (bf16[32,4096]{1,0:T(8,128)(2,1)S(1)}, bf16[32,4096]{1,0:T(8,128)(2,1)S(1)}, u32[]{:S(2)}, u32[]{:S(2)}) collective-permute-start(bf16[32,4096]{1,0:T(8,128)(2,1)S(1)} %reshape.211), channel_id=1, source_target_pairs={{0,96},{1,25},{8,104},{9,1},{16,112},{17,9},{24,120},{25,17},{32,0... | collective-permute-start | bytes 786440 | tf_op jit(solution)/shard_map/ppermute | solution.py:41
  79.9 5.4 %collective-permute-done.19 = bf16[32,4096]{1,0:T(8,128)(2,1)S(1)} collective-permute-done((bf16[32,4096]{1,0:T(8,128)(2,1)S(1)}, bf16[32,4096]{1,0:T(8,128)(2,1)S(1)}, u32[]{:S(2)}, u32[]{:S(2)}) %collective-permute-start.19) | collective-permute-done | bytes 262176 | tf_op jit(solution)/shard_map/ppermute | solution.py:41
  86.2 2.8 %collective-permute-done.17 = bf16[32,4096]{1,0:T(8,128)(2,1)S(1)} collective-permute-done((bf16[32,4096]{1,0:T(8,128)(2,1)S(1)}, bf16[32,4096]{1,0:T(8,128)(2,1)S(1)}, u32[]{:S(2)}, u32[]{:S(2)}) %collective-permute-start.17) | collective-permute-done | bytes 262176 | tf_op jit(solution)/shard_map/ppermute | solution.py:41
  89.1 1.3 collective-permute-start.21
  90.7 7.3 %load_weights.1 = (bf16[4096,896]{1,0:T(8,128)(2,1)S(1)}, bf16[4096,896]{1,0:T(8,128)(2,1)S(1)}, bf16[896,4096]{1,0:T(8,128)(2,1)S(1)}) custom-call(bf16[4096,896]{1,0:T(8,128)(2,1)} %bitcast.102, bf16[4096,896]{1,0:T(8,128)(2,1)} %bitcast.103, bf16[896,4096]{1,0:T(8,128)(2,1)} %bitcast.104, bf16[4,32,4096]{2,1,0:T(8,128)(2,1)S(1)} %pad_maximum_fusion.refs_3_), custom_call_target="tpu_custom_call" | custom-call | tf_op jit(solution)/shard_map/load_weights/pallas_call | solution.py:247
  97.9 3.5 %expert_rows.4.refs_4_ = bf16[128,4096]{1,0:T(8,128)(2,1)S(1)} custom-call(bf16[128,4096]{1,0:T(8,128)(2,1)S(1)} %bitcast.100, bf16[4096,896]{1,0:T(8,128)(2,1)S(1)} %get-tuple-element.28.refs_1_.refs_2_, bf16[4096,896]{1,0:T(8,128)(2,1)S(1)} %get-tuple-element.29.refs_2_.refs_3_, bf16[896,4096]{1,0:T(8,128)(2,1)S(1)} %get-tuple-element.30.refs_3_.refs_4_, ...), custom_call_target="tpu_custom_call" | custom-call | tf_op jit(solution)/shard_map/expert_rows/pallas_call | solution.py:189
  101.5 1.7 collective-permute-done.21.refs_0_
  103.1 2.4 %collective-permute-done.20.refs_0_ = bf16[128,4096]{1,0:T(8,128)(2,1)S(1)} collective-permute-done((bf16[128,4096]{1,0:T(8,128)(2,1)S(1)}, bf16[128,4096]{1,0:T(8,128)(2,1)S(1)}, u32[]{:S(2)}, u32[]{:S(2)}) %collective-permute-start.20) | collective-permute-done | bytes 1048608 | tf_op jit(solution)/shard_map/ppermute | solution.py:41
  105.6 1.2 collective-permute-start.23
  107.1 3.5 %expert_rows.5.refs_4_ = bf16[128,4096]{1,0:T(8,128)(2,1)S(1)} custom-call(bf16[128,4096]{1,0:T(8,128)(2,1)S(1)} %collective-permute-done.20.refs_0_, bf16[4096,896]{1,0:T(8,128)(2,1)S(1)} %get-tuple-element.28.refs_1_.refs_2_, bf16[4096,896]{1,0:T(8,128)(2,1)S(1)} %get-tuple-element.29.refs_2_.refs_3_, ...), custom_call_target="tpu_custom_call" | custom-call | tf_op jit(solution)/shard_map/expert_rows/pallas_call | solution.py:189
  110.7 3.5 %expert_rows.6.refs_5_ = bf16[128,4096]{1,0:T(8,128)(2,1)S(1)} custom-call(bf16[128,4096]{1,0:T(8,128)(2,1)S(1)} %collective-permute-done.21.refs_0_, bf16[4096,896]{1,0:T(8,128)(2,1)S(1)} %get-tuple-element.28.refs_1_.refs_2_, bf16[4096,896]{1,0:T(8,128)(2,1)S(1)} %get-tuple-element.29.refs_2_.refs_3_, ...), custom_call_target="tpu_custom_call" | custom-call | tf_op jit(solution)/shard_map/expert_rows/pallas_call | solution.py:189
  114.2 2.2 %collective-permute-done.22.refs_0_ = bf16[64,4096]{1,0:T(8,128)(2,1)S(1)} collective-permute-done((bf16[64,4096]{1,0:T(8,128)(2,1)S(1)}, bf16[64,4096]{1,0:T(8,128)(2,1)S(1)}, u32[]{:S(2)}, u32[]{:S(2)}) %collective-permute-start.22) | collective-permute-done | bytes 524320 | tf_op jit(solution)/shard_map/ppermute | solution.py:41
  116.4 3.5 %expert_rows.7 = (bf16[64,4096]{1,0:T(8,128)(2,1)S(1)}, bf16[64,4096]{1,0:T(8,128)(2,1)S(1)}) custom-call(bf16[64,4096]{1,0:T(8,128)(2,1)S(1)} %collective-permute-done.22.refs_0_, bf16[64,4096]{1,0:T(8,128)(2,1)S(1)} %collective-permute-done.23.refs_1_, bf16[4096,896]{1,0:T(8,128)(2,1)S(1)} %get-tuple-element.28.refs_1_.refs_2_, ...), custom_call_target="tpu_custom_call" | custom-call | tf_op jit(solution)/shard_map/expert_rows/pallas_call | solution.py:189
  120.0 2.7 %collective-permute-start.24 = (bf16[64,4096]{1,0:T(8,128)(2,1)S(1)}, bf16[64,4096]{1,0:T(8,128)(2,1)S(1)}, u32[]{:S(2)}, u32[]{:S(2)}) collective-permute-start(bf16[64,4096]{1,0:T(8,128)(2,1)S(1)} %get-tuple-element.34), channel_id=1, source_target_pairs={{0,24},{1,97},{8,0},{9,105},{16,8},{17,113},{24,16},{25,121},{32,5... | collective-permute-start | bytes 1572872 | tf_op jit(solution)/shard_map/ppermute | solution.py:41
  122.6 6.9 %collective-permute-done.26 = bf16[64,4096]{1,0:T(8,128)(2,1)S(1)} collective-permute-done((bf16[64,4096]{1,0:T(8,128)(2,1)S(1)}, bf16[64,4096]{1,0:T(8,128)(2,1)S(1)}, u32[]{:S(2)}, u32[]{:S(2)}) %collective-permute-start.26) | collective-permute-done | bytes 524320 | tf_op jit(solution)/shard_map/ppermute | solution.py:41
  130.0 3.0 %collective-permute-start.25 = (bf16[128,4096]{1,0:T(8,128)(2,1)S(1)}, bf16[128,4096]{1,0:T(8,128)(2,1)S(1)}, u32[]{:S(2)}, u32[]{:S(2)}) collective-permute-start(bf16[128,4096]{1,0:T(8,128)(2,1)S(1)} %pad_maximum_fusion.1), channel_id=1, source_target_pairs={{0,24},{1,97},{8,0},{9,105},{16,8},{17,113},{24,16},{25,121},{32,5... | collective-permute-start | bytes 3145736 | tf_op jit(solution)/shard_map/ppermute | solution.py:41
  133.0 12.0 %collective-permute-done.27 = bf16[128,4096]{1,0:T(8,128)(2,1)S(1)} collective-permute-done((bf16[128,4096]{1,0:T(8,128)(2,1)S(1)}, bf16[128,4096]{1,0:T(8,128)(2,1)S(1)}, u32[]{:S(2)}, u32[]{:S(2)}) %collective-permute-start.27) | collective-permute-done | bytes 1048608 | tf_op jit(solution)/shard_map/ppermute | solution.py:41
  147.7 4.7 %collective-permute-done.28 = bf16[32,4096]{1,0:T(8,128)(2,1)S(1)} collective-permute-done((bf16[32,4096]{1,0:T(8,128)(2,1)S(1)}, bf16[32,4096]{1,0:T(8,128)(2,1)S(1)}, u32[]{:S(2)}, u32[]{:S(2)}) %collective-permute-start.28) | collective-permute-done | bytes 262176 | tf_op jit(solution)/shard_map/ppermute | solution.py:41
  152.4 3.5 %collective-permute-done.30 = bf16[32,4096]{1,0:T(8,128)(2,1)S(1)} collective-permute-done((bf16[32,4096]{1,0:T(8,128)(2,1)S(1)}, bf16[32,4096]{1,0:T(8,128)(2,1)S(1)}, u32[]{:S(2)}, u32[]{:S(2)}) %collective-permute-start.30) | collective-permute-done | bytes 262176 | tf_op jit(solution)/shard_map/ppermute | solution.py:41
  157.7 1.6 collective-permute-done.31
  159.3 2.0 %collective-permute-done.32 = bf16[2,4,4096]{2,1,0:T(4,128)(2,1)S(1)} collective-permute-done((bf16[2,4,4096]{2,1,0:T(4,128)(2,1)S(1)}, bf16[2,4,4096]{2,1,0:T(4,128)(2,1)S(1)}, u32[]{:S(2)}, u32[]{:S(2)}) %collective-permute-start.32) | collective-permute-done | bytes 65568 | tf_op jit(solution)/shard_map/ppermute | solution.py:27
  162.6 14.1 %collective-permute-start.34 = (bf16[4,4,4096]{2,1,0:T(4,128)(2,1)S(1)}, bf16[4,4,4096]{2,1,0:T(4,128)(2,1)S(1)}, u32[]{:S(2)}, u32[]{:S(2)}) collective-permute-start(bf16[4,4,4096]{2,1,0:T(4,128)(2,1)S(1)} %get-tuple-element.47), channel_id=1, source_target_pairs={{0,1},{1,0},{2,3},{3,2},{4,5},{5,4},{6,7},{7,6},{8,9},{9,8},{10,11... | collective-permute-start | bytes 393224 | tf_op jit(solution)/shard_map/ppermute | solution.py:45
  (129 shorter events, 21.8 us)
Async XLA Ops:
  0.6 36.1 %copy-start = (bf16[64,64,128]{2,1,0:T(8,128)(2,1)S(1)}, bf16[64,64,128]{2,1,0:T(8,128)(2,1)}, u32[]{:S(2)}) copy-start(bf16[64,64,128]{2,1,0:T(8,128)(2,1)} %param.22) | copy-start | bytes 3145732
  2.6 15.9 %all-to-all-start = ((bf16[16,16,512]{2,1,0:T(8,128)(2,1)}), bf16[16,16,512]{2,1,0:T(8,128)(2,1)S(1)}, u32[]{:S(2)}, u32[]{:S(2)}) async-start(bf16[16,16,512]{2,1,0:T(8,128)(2,1)} %bitcast.4), calls=%async_computation | async-start | bytes 524288 | tf_op jit(solution)/shard_map/all_to_all | solution.py:289
  13.4 15.2 %copy-start.2 = (bf16[512,256]{1,0:T(8,128)(2,1)S(1)}, bf16[512,256]{1,0:T(8,128)(2,1)}, u32[]{:S(2)}) copy-start(bf16[512,256]{1,0:T(8,128)(2,1)} %refs_4_.1) | copy-start | bytes 786436
  23.5 12.3 %all-to-all-start.1 = ((bf16[16,16,640]{2,1,0:T(8,128)(2,1)}), bf16[16,16,640]{2,1,0:T(8,128)(2,1)S(1)}, u32[]{:S(2)}, u32[]{:S(2)}) async-start(bf16[16,16,640]{2,1,0:T(8,128)(2,1)} %bitcast.7), calls=%async_computation.1 | async-start | bytes 655360 | tf_op jit(solution)/shard_map/all_to_all | solution.py:298
  28.6 11.9 %collective-permute-start.5 = (bf16[512,256]{1,0:T(8,128)(2,1)S(1)}, bf16[512,256]{1,0:T(8,128)(2,1)S(1)}, u32[]{:S(2)}, u32[]{:S(2)}) collective-permute-start(bf16[512,256]{1,0:T(8,128)(2,1)S(1)} %copy-done.2), channel_id=1, source_target_pairs={{0,32},{32,64},{64,96},{96,0},{1,33},{33,65},{65,97},{97,1},{2,34}... | collective-permute-start | bytes 786440 | tf_op jit(solution)/shard_map/ppermute | solution.py:27
  29.9 15.2 %collective-permute-start.4 = (bf16[512,256]{1,0:T(8,128)(2,1)S(1)}, bf16[512,256]{1,0:T(8,128)(2,1)S(1)}, u32[]{:S(2)}, u32[]{:S(2)}) collective-permute-start(bf16[512,256]{1,0:T(8,128)(2,1)S(1)} %copy-done.2), channel_id=1, source_target_pairs={{0,64},{32,96},{64,0},{96,32},{1,65},{33,97},{65,1},{97,33},{2,66}... | collective-permute-start | bytes 786440 | tf_op jit(solution)/shard_map/ppermute | solution.py:27
  32.3 12.8 %collective-permute-start.3 = (bf16[512,256]{1,0:T(8,128)(2,1)S(1)}, bf16[512,256]{1,0:T(8,128)(2,1)S(1)}, u32[]{:S(2)}, u32[]{:S(2)}) collective-permute-start(bf16[512,256]{1,0:T(8,128)(2,1)S(1)} %copy-done.2), channel_id=1, source_target_pairs={{0,96},{32,0},{64,32},{96,64},{1,97},{33,1},{65,33},{97,65},{2,98}... | collective-permute-start | bytes 786440 | tf_op jit(solution)/shard_map/ppermute | solution.py:27
  36.0 5.7 %copy-start.5 = (s32[8,2]{0,1:T(2,128)S(1)}, s32[8,2]{0,1:T(2,128)}, u32[]{:S(2)}) copy-start(s32[8,2]{0,1:T(2,128)} %param.31) | copy-start | bytes 196
  37.2 26.3 %copy-start.4 = (bf16[8,4096]{1,0:T(8,128)(2,1)S(1)}, bf16[8,4096]{1,0:T(8,128)(2,1)}, u32[]{:S(2)}) copy-start(bf16[8,4096]{1,0:T(8,128)(2,1)} %param.29) | copy-start | bytes 196612
  37.2 26.4 %copy-start.3 = (f32[4096]{0:T(1024)S(1)}, f32[4096]{0:T(1024)}, u32[]{:S(2)}) copy-start(f32[4096]{0:T(1024)} %refs_4_.2) | copy-start | bytes 49156
  37.3 7.9 %collective-permute-start.2 = (bf16[2,32,512]{2,1,0:T(8,128)(2,1)S(1)}, bf16[2,32,512]{2,1,0:T(8,128)(2,1)S(1)}, u32[]{:S(2)}, u32[]{:S(2)}) collective-permute-start(bf16[2,32,512]{2,1,0:T(8,128)(2,1)S(1)} %fusion.18.refs_0_), channel_id=1, source_target_pairs={{0,24},{8,0},{16,8},{24,16},{1,25},{9,1},{17,9},{25,17},{2,26},{10... | collective-permute-start | bytes 196616 | tf_op jit(solution)/shard_map/ppermute | solution.py:27
  38.1 7.0 %collective-permute-start.1 = (bf16[2,32,512]{2,1,0:T(8,128)(2,1)S(1)}, bf16[2,32,512]{2,1,0:T(8,128)(2,1)S(1)}, u32[]{:S(2)}, u32[]{:S(2)}) collective-permute-start(bf16[2,32,512]{2,1,0:T(8,128)(2,1)S(1)} %fusion.18.refs_0_), channel_id=1, source_target_pairs={{0,16},{8,24},{16,0},{24,8},{1,17},{9,25},{17,1},{25,9},{2,18},{10... | collective-permute-start | bytes 196616 | tf_op jit(solution)/shard_map/ppermute | solution.py:27
  40.5 4.7 %collective-permute-start = (bf16[2,32,512]{2,1,0:T(8,128)(2,1)S(1)}, bf16[2,32,512]{2,1,0:T(8,128)(2,1)S(1)}, u32[]{:S(2)}, u32[]{:S(2)}) collective-permute-start(bf16[2,32,512]{2,1,0:T(8,128)(2,1)S(1)} %fusion.18.refs_0_), channel_id=1, source_target_pairs={{0,8},{8,16},{16,24},{24,0},{1,9},{9,17},{17,25},{25,1},{2,10},{10... | collective-permute-start | bytes 196616 | tf_op jit(solution)/shard_map/ppermute | solution.py:27
  45.7 5.2 %collective-permute-start.6 = (bf16[4,4,8,1024]{3,2,1,0:T(8,128)(2,1)S(1)}, bf16[4,4,8,1024]{3,2,1,0:T(8,128)(2,1)S(1)}, u32[]{:S(2)}, u32[]{:S(2)}) collective-permute-start(bf16[4,4,8,1024]{3,2,1,0:T(8,128)(2,1)S(1)} %get-tuple-element.24), channel_id=1, source_target_pairs={{0,1},{1,0},{2,3},{3,2},{4,5},{5,4},{6,7},{7,6},{8,9},{9,8},{10,11... | collective-permute-start | bytes 786440 | tf_op jit(solution)/shard_map/ppermute | solution.py:45
  50.9 4.5 %collective-permute-start.7 = (bf16[4,8,1024]{2,1,0:T(8,128)(2,1)S(1)}, bf16[4,8,1024]{2,1,0:T(8,128)(2,1)S(1)}, u32[]{:S(2)}, u32[]{:S(2)}) collective-permute-start(bf16[4,8,1024]{2,1,0:T(8,128)(2,1)S(1)} %get-tuple-element.58), channel_id=1, source_target_pairs={{0,2},{2,4},{4,6},{6,0},{1,3},{3,5},{5,7},{7,1},{8,10},{10,12},{12... | collective-permute-start | bytes 196616 | tf_op jit(solution)/shard_map/ppermute | solution.py:27
  52.2 3.2 %collective-permute-start.9 = (bf16[4,8,1024]{2,1,0:T(8,128)(2,1)S(1)}, bf16[4,8,1024]{2,1,0:T(8,128)(2,1)S(1)}, u32[]{:S(2)}, u32[]{:S(2)}) collective-permute-start(bf16[4,8,1024]{2,1,0:T(8,128)(2,1)S(1)} %get-tuple-element.59), channel_id=1, source_target_pairs={{0,6},{2,0},{4,2},{6,4},{1,7},{3,1},{5,3},{7,5},{8,14},{10,8},{12,... | collective-permute-start | bytes 196616 | tf_op jit(solution)/shard_map/ppermute | solution.py:27
  53.7 4.6 %collective-permute-start.8 = (bf16[4,8,1024]{2,1,0:T(8,128)(2,1)S(1)}, bf16[4,8,1024]{2,1,0:T(8,128)(2,1)S(1)}, u32[]{:S(2)}, u32[]{:S(2)}) collective-permute-start(bf16[4,8,1024]{2,1,0:T(8,128)(2,1)S(1)} %get-tuple-element.60), channel_id=1, source_target_pairs={{0,4},{2,6},{4,0},{6,2},{1,5},{3,7},{5,1},{7,3},{8,12},{10,14},{12... | collective-permute-start | bytes 196616 | tf_op jit(solution)/shard_map/ppermute | solution.py:27
  58.4 4.8 %collective-permute-start.12 = (bf16[8,1024]{1,0:T(8,128)(2,1)S(1)}, bf16[8,1024]{1,0:T(8,128)(2,1)S(1)}, u32[]{:S(2)}, u32[]{:S(2)}) collective-permute-start(bf16[8,1024]{1,0:T(8,128)(2,1)S(1)} %get-tuple-element.61), channel_id=1, source_target_pairs={{0,8},{8,16},{16,24},{24,0},{1,9},{9,17},{17,25},{25,1},{2,10},{10... | collective-permute-start | bytes 49160 | tf_op jit(solution)/shard_map/ppermute | solution.py:27
  58.5 4.7 %collective-permute-start.11 = (bf16[8,1024]{1,0:T(8,128)(2,1)S(1)}, bf16[8,1024]{1,0:T(8,128)(2,1)S(1)}, u32[]{:S(2)}, u32[]{:S(2)}) collective-permute-start(bf16[8,1024]{1,0:T(8,128)(2,1)S(1)} %get-tuple-element.62), channel_id=1, source_target_pairs={{0,16},{8,24},{16,0},{24,8},{1,17},{9,25},{17,1},{25,9},{2,18},{10... | collective-permute-start | bytes 49160 | tf_op jit(solution)/shard_map/ppermute | solution.py:27
  60.7 2.6 %collective-permute-start.10 = (bf16[8,1024]{1,0:T(8,128)(2,1)S(1)}, bf16[8,1024]{1,0:T(8,128)(2,1)S(1)}, u32[]{:S(2)}, u32[]{:S(2)}) collective-permute-start(bf16[8,1024]{1,0:T(8,128)(2,1)S(1)} %get-tuple-element.63), channel_id=1, source_target_pairs={{0,24},{8,0},{16,8},{24,16},{1,25},{9,1},{17,9},{25,17},{2,26},{10... | collective-permute-start | bytes 49160 | tf_op jit(solution)/shard_map/ppermute | solution.py:27
  64.1 4.7 %collective-permute-start.13 = (bf16[4,4,4096]{2,1,0:T(4,128)(2,1)S(1)}, bf16[4,4,4096]{2,1,0:T(4,128)(2,1)S(1)}, u32[]{:S(2)}, u32[]{:S(2)}) collective-permute-start(bf16[4,4,4096]{2,1,0:T(4,128)(2,1)S(1)} %get-tuple-element.57), channel_id=1, source_target_pairs={{0,1},{1,0},{2,3},{3,2},{4,5},{5,4},{6,7},{7,6},{8,9},{9,8},{10,11... | collective-permute-start | bytes 393224 | tf_op jit(solution)/shard_map/ppermute | solution.py:45
  69.0 4.4 %collective-permute-start.14 = (bf16[2,4,4096]{2,1,0:T(4,128)(2,1)S(1)}, bf16[2,4,4096]{2,1,0:T(4,128)(2,1)S(1)}, u32[]{:S(2)}, u32[]{:S(2)}) collective-permute-start(bf16[2,4,4096]{2,1,0:T(4,128)(2,1)S(1)} %get-tuple-element.53), channel_id=1, source_target_pairs={{0,2},{2,4},{4,6},{6,0},{1,3},{3,5},{5,7},{7,1},{8,10},{10,12},{12... | collective-permute-start | bytes 196616 | tf_op jit(solution)/shard_map/ppermute | solution.py:27
  69.2 4.2 %collective-permute-start.16 = (bf16[2,4,4096]{2,1,0:T(4,128)(2,1)S(1)}, bf16[2,4,4096]{2,1,0:T(4,128)(2,1)S(1)}, u32[]{:S(2)}, u32[]{:S(2)}) collective-permute-start(bf16[2,4,4096]{2,1,0:T(4,128)(2,1)S(1)} %get-tuple-element.54), channel_id=1, source_target_pairs={{0,6},{2,0},{4,2},{6,4},{1,7},{3,1},{5,3},{7,5},{8,14},{10,8},{12,... | collective-permute-start | bytes 196616 | tf_op jit(solution)/shard_map/ppermute | solution.py:27
  71.8 4.6 %collective-permute-start.15 = (bf16[2,4,4096]{2,1,0:T(4,128)(2,1)S(1)}, bf16[2,4,4096]{2,1,0:T(4,128)(2,1)S(1)}, u32[]{:S(2)}, u32[]{:S(2)}) collective-permute-start(bf16[2,4,4096]{2,1,0:T(4,128)(2,1)S(1)} %get-tuple-element.55), channel_id=1, source_target_pairs={{0,4},{2,6},{4,0},{6,2},{1,5},{3,7},{5,1},{7,3},{8,12},{10,14},{12... | collective-permute-start | bytes 196616 | tf_op jit(solution)/shard_map/ppermute | solution.py:27
  76.7 8.6 %collective-permute-start.19 = (bf16[32,4096]{1,0:T(8,128)(2,1)S(1)}, bf16[32,4096]{1,0:T(8,128)(2,1)S(1)}, u32[]{:S(2)}, u32[]{:S(2)}) collective-permute-start(bf16[32,4096]{1,0:T(8,128)(2,1)S(1)} %reshape.211), channel_id=1, source_target_pairs={{0,96},{1,25},{8,104},{9,1},{16,112},{17,9},{24,120},{25,17},{32,0... | collective-permute-start | bytes 786440 | tf_op jit(solution)/shard_map/ppermute | solution.py:41
  79.2 7.1 %collective-permute-start.18 = (bf16[32,4096]{1,0:T(8,128)(2,1)S(1)}, bf16[32,4096]{1,0:T(8,128)(2,1)S(1)}, u32[]{:S(2)}, u32[]{:S(2)}) collective-permute-start(bf16[32,4096]{1,0:T(8,128)(2,1)S(1)} %reshape.211), channel_id=1, source_target_pairs={{0,64},{1,17},{8,72},{9,25},{16,80},{17,1},{24,88},{25,9},{32,96},... | collective-permute-start | bytes 786440 | tf_op jit(solution)/shard_map/ppermute | solution.py:41
  79.6 9.3 %collective-permute-start.17 = (bf16[32,4096]{1,0:T(8,128)(2,1)S(1)}, bf16[32,4096]{1,0:T(8,128)(2,1)S(1)}, u32[]{:S(2)}, u32[]{:S(2)}) collective-permute-start(bf16[32,4096]{1,0:T(8,128)(2,1)S(1)} %reshape.211), channel_id=1, source_target_pairs={{0,32},{1,9},{8,40},{9,17},{16,48},{17,25},{24,56},{25,1},{32,64},... | collective-permute-start | bytes 786440 | tf_op jit(solution)/shard_map/ppermute | solution.py:41
  89.1 14.0 %collective-permute-start.21 = (bf16[128,4096]{1,0:T(8,128)(2,1)S(1)}, bf16[128,4096]{1,0:T(8,128)(2,1)S(1)}, u32[]{:S(2)}, u32[]{:S(2)}) collective-permute-start(bf16[128,4096]{1,0:T(8,128)(2,1)S(1)} %bitcast.98), channel_id=1, source_target_pairs={{0,24},{1,97},{8,0},{9,105},{16,8},{17,113},{24,16},{25,121},{32,5... | collective-permute-start | bytes 3145736 | tf_op jit(solution)/shard_map/ppermute | solution.py:41
  90.4 15.2 %collective-permute-start.20 = (bf16[128,4096]{1,0:T(8,128)(2,1)S(1)}, bf16[128,4096]{1,0:T(8,128)(2,1)S(1)}, u32[]{:S(2)}, u32[]{:S(2)}) collective-permute-start(bf16[128,4096]{1,0:T(8,128)(2,1)S(1)} %bitcast.99), channel_id=1, source_target_pairs={{0,8},{1,33},{8,16},{9,41},{16,24},{17,49},{24,0},{25,57},{32,40},... | collective-permute-start | bytes 3145736 | tf_op jit(solution)/shard_map/ppermute | solution.py:41
  105.6 8.5 %collective-permute-start.23 = (bf16[64,4096]{1,0:T(8,128)(2,1)S(1)}, bf16[64,4096]{1,0:T(8,128)(2,1)S(1)}, u32[]{:S(2)}, u32[]{:S(2)}) collective-permute-start(bf16[64,4096]{1,0:T(8,128)(2,1)S(1)} %slice.124), channel_id=1, source_target_pairs={{0,24},{1,97},{8,0},{9,105},{16,8},{17,113},{24,16},{25,121},{32,5... | collective-permute-start | bytes 1572872 | tf_op jit(solution)/shard_map/ppermute | solution.py:41
  106.8 9.5 %collective-permute-start.22 = (bf16[64,4096]{1,0:T(8,128)(2,1)S(1)}, bf16[64,4096]{1,0:T(8,128)(2,1)S(1)}, u32[]{:S(2)}, u32[]{:S(2)}) collective-permute-start(bf16[64,4096]{1,0:T(8,128)(2,1)S(1)} %slice.123), channel_id=1, source_target_pairs={{0,8},{1,33},{8,16},{9,41},{16,24},{17,49},{24,0},{25,57},{32,40},... | collective-permute-start | bytes 1572872 | tf_op jit(solution)/shard_map/ppermute | solution.py:41
  119.9 9.6 %collective-permute-start.26 = (bf16[64,4096]{1,0:T(8,128)(2,1)S(1)}, bf16[64,4096]{1,0:T(8,128)(2,1)S(1)}, u32[]{:S(2)}, u32[]{:S(2)}) collective-permute-start(bf16[64,4096]{1,0:T(8,128)(2,1)S(1)} %get-tuple-element.35), channel_id=1, source_target_pairs={{0,8},{1,33},{8,16},{9,41},{16,24},{17,49},{24,0},{25,57},{32,40},... | collective-permute-start | bytes 1572872 | tf_op jit(solution)/shard_map/ppermute | solution.py:41
  120.0 9.8 %collective-permute-start.24 = (bf16[64,4096]{1,0:T(8,128)(2,1)S(1)}, bf16[64,4096]{1,0:T(8,128)(2,1)S(1)}, u32[]{:S(2)}, u32[]{:S(2)}) collective-permute-start(bf16[64,4096]{1,0:T(8,128)(2,1)S(1)} %get-tuple-element.34), channel_id=1, source_target_pairs={{0,24},{1,97},{8,0},{9,105},{16,8},{17,113},{24,16},{25,121},{32,5... | collective-permute-start | bytes 1572872 | tf_op jit(solution)/shard_map/ppermute | solution.py:41
  129.7 15.2 %collective-permute-start.27 = (bf16[128,4096]{1,0:T(8,128)(2,1)S(1)}, bf16[128,4096]{1,0:T(8,128)(2,1)S(1)}, u32[]{:S(2)}, u32[]{:S(2)}) collective-permute-start(bf16[128,4096]{1,0:T(8,128)(2,1)S(1)} %pad_maximum_fusion.2), channel_id=1, source_target_pairs={{0,8},{1,33},{8,16},{9,41},{16,24},{17,49},{24,0},{25,57},{32,40},... | collective-permute-start | bytes 3145736 | tf_op jit(solution)/shard_map/ppermute | solution.py:41
  130.0 14.9 %collective-permute-start.25 = (bf16[128,4096]{1,0:T(8,128)(2,1)S(1)}, bf16[128,4096]{1,0:T(8,128)(2,1)S(1)}, u32[]{:S(2)}, u32[]{:S(2)}) collective-permute-start(bf16[128,4096]{1,0:T(8,128)(2,1)S(1)} %pad_maximum_fusion.1), channel_id=1, source_target_pairs={{0,24},{1,97},{8,0},{9,105},{16,8},{17,113},{24,16},{25,121},{32,5... | collective-permute-start | bytes 3145736 | tf_op jit(solution)/shard_map/ppermute | solution.py:41
  145.5 31.3 %copy-start.6 = (f32[8,2]{0,1:T(2,128)S(1)}, f32[8,2]{0,1:T(2,128)}, u32[]{:S(2)}) copy-start(f32[8,2]{0,1:T(2,128)} %param.32) | copy-start | bytes 196
  145.5 6.9 %collective-permute-start.28 = (bf16[32,4096]{1,0:T(8,128)(2,1)S(1)}, bf16[32,4096]{1,0:T(8,128)(2,1)S(1)}, u32[]{:S(2)}, u32[]{:S(2)}) collective-permute-start(bf16[32,4096]{1,0:T(8,128)(2,1)S(1)} %get-tuple-element.39), channel_id=1, source_target_pairs={{0,96},{1,25},{8,104},{9,1},{16,112},{17,9},{24,120},{25,17},{32,0... | collective-permute-start | bytes 786440 | tf_op jit(solution)/shard_map/ppermute | solution.py:41
  145.9 10.0 %collective-permute-start.30 = (bf16[32,4096]{1,0:T(8,128)(2,1)S(1)}, bf16[32,4096]{1,0:T(8,128)(2,1)S(1)}, u32[]{:S(2)}, u32[]{:S(2)}) collective-permute-start(bf16[32,4096]{1,0:T(8,128)(2,1)S(1)} %get-tuple-element.40), channel_id=1, source_target_pairs={{0,32},{1,9},{8,40},{9,17},{16,48},{17,25},{24,56},{25,1},{32,64},... | collective-permute-start | bytes 786440 | tf_op jit(solution)/shard_map/ppermute | solution.py:41
  147.0 8.9 %collective-permute-start.29 = (bf16[32,4096]{1,0:T(8,128)(2,1)S(1)}, bf16[32,4096]{1,0:T(8,128)(2,1)S(1)}, u32[]{:S(2)}, u32[]{:S(2)}) collective-permute-start(bf16[32,4096]{1,0:T(8,128)(2,1)S(1)} %get-tuple-element.41), channel_id=1, source_target_pairs={{0,64},{1,17},{8,72},{9,25},{16,80},{17,1},{24,88},{25,9},{32,96},... | collective-permute-start | bytes 786440 | tf_op jit(solution)/shard_map/ppermute | solution.py:41
  155.9 22.9 %copy-start.1 = (bf16[64,64,128]{2,1,0:T(8,128)(2,1)S(1)}, bf16[64,64,128]{2,1,0:T(8,128)(2,1)}, u32[]{:S(2)}) copy-start(bf16[64,64,128]{2,1,0:T(8,128)(2,1)} %param.22) | copy-start | bytes 3145732
  156.1 3.2 %collective-permute-start.31 = (bf16[2,4,4096]{2,1,0:T(4,128)(2,1)S(1)}, bf16[2,4,4096]{2,1,0:T(4,128)(2,1)S(1)}, u32[]{:S(2)}, u32[]{:S(2)}) collective-permute-start(bf16[2,4,4096]{2,1,0:T(4,128)(2,1)S(1)} %squeeze.60), channel_id=1, source_target_pairs={{0,6},{2,0},{4,2},{6,4},{1,7},{3,1},{5,3},{7,5},{8,14},{10,8},{12,... | collective-permute-start | bytes 196616 | tf_op jit(solution)/shard_map/ppermute | solution.py:27
  156.7 4.6 %collective-permute-start.32 = (bf16[2,4,4096]{2,1,0:T(4,128)(2,1)S(1)}, bf16[2,4,4096]{2,1,0:T(4,128)(2,1)S(1)}, u32[]{:S(2)}, u32[]{:S(2)}) collective-permute-start(bf16[2,4,4096]{2,1,0:T(4,128)(2,1)S(1)} %squeeze.61), channel_id=1, source_target_pairs={{0,4},{2,6},{4,0},{6,2},{1,5},{3,7},{5,1},{7,3},{8,12},{10,14},{12... | collective-permute-start | bytes 196616 | tf_op jit(solution)/shard_map/ppermute | solution.py:27
  156.9 5.4 %collective-permute-start.33 = (bf16[2,4,4096]{2,1,0:T(4,128)(2,1)S(1)}, bf16[2,4,4096]{2,1,0:T(4,128)(2,1)S(1)}, u32[]{:S(2)}, u32[]{:S(2)}) collective-permute-start(bf16[2,4,4096]{2,1,0:T(4,128)(2,1)S(1)} %squeeze.62), channel_id=1, source_target_pairs={{0,2},{2,4},{4,6},{6,0},{1,3},{3,5},{5,7},{7,1},{8,10},{10,12},{12... | collective-permute-start | bytes 196616 | tf_op jit(solution)/shard_map/ppermute | solution.py:27
  162.6 15.1 %collective-permute-start.34 = (bf16[4,4,4096]{2,1,0:T(4,128)(2,1)S(1)}, bf16[4,4,4096]{2,1,0:T(4,128)(2,1)S(1)}, u32[]{:S(2)}, u32[]{:S(2)}) collective-permute-start(bf16[4,4,4096]{2,1,0:T(4,128)(2,1)S(1)} %get-tuple-element.47), channel_id=1, source_target_pairs={{0,1},{1,0},{2,3},{3,2},{4,5},{5,4},{6,7},{7,6},{8,9},{9,8},{10,11... | collective-permute-start | bytes 393224 | tf_op jit(solution)/shard_map/ppermute | solution.py:45
